TPU v7x, 32 devices: a whole 2x2x4 slice. The times are simulated.
32 devices in a mesh: dp: 4 (over z), tensor: 8 (over y, x, core).
Axes of the slice: x: 2, y: 2, z: 4, core: 2. Of those that a mesh axis runs over, the one named last changes fastest.
Arguments:
- embed_rows: bfloat16 [98304, 512], P('tensor', 'dp'), may hold values from -6 to 6
- head_rows: bfloat16 [98304, 512], P('tensor', 'dp'), may hold values from -6 to 6
- row_offsets: int32 [2, 9], replicated, may hold values from -2047 to 67583, as said below
- slot_table: int32 [1024], replicated, may hold values from 0 to 1023, as said below
- probe: bfloat16 [512, 1024], replicated, may hold values from -0.25 to 0.25
Outputs:
- stored: bfloat16 [1024, 128, 512], P(('dp', 'tensor'))
- sketch: float32 [1024, 128, 1024], P(('dp', 'tensor'))
Inputs may be any that keep to these rules, and one draw needn't show every extreme that they name: row_offsets[m, 8] is row_offsets[m, 0] + 65536; every entry row_offsets[m, t] with t < 8 lies strictly within 2048 rows of t * 8192, and the distance 8192 // 4 - 1 is reached above and below among ranks 1 onward in every row of every draw; row_offsets[m, 0] is never 0, above 0 for one matrix and below 0 for the other. `slot_table`: A permutation of the 1024 block numbers. Devices along dp+tensor write 32 consecutive slots each; among one device's slots exactly 4 blocks come from each aligned range of 8192 vocabulary rows (rows t * 8192 onward of either matrix, both matrices together).
All inputs are finite; a program needn't handle non-finite values.
Results may differ from a plain program's by a relative error of at most 0.001.
Values may be sent and summed in bfloat16 or wider, within the bound.
A program may use at most 64 MiB of HBM per device.

v0:
```python
import functools

import jax
import jax.numpy as jnp
from jax import lax
from jax.experimental import pallas as pl
from jax.experimental.pallas import tpu as pltpu
from jax.sharding import PartitionSpec as P

R = 8192
BLOCK = 128
TILE = 16
WINDOW = 256
MIB = 1 << 20


def from_behind(block, axis, distance):
    devices = range(lax.axis_size(axis))
    route = [((i - distance) % len(devices), i) for i in devices]
    return lax.ppermute(block, axis, route)


def floor_tile(value):
    return lax.shift_left(lax.shift_right_arithmetic(value, 4), 4)


def tail_begin(offset, rank, height, quarter):
    return jnp.clip((rank + 1) * R - offset, 0, height - quarter - 1)


def selector(offset):
    row = lax.broadcasted_iota(jnp.int32, (BLOCK, WINDOW), 0)
    column = lax.broadcasted_iota(jnp.int32, (BLOCK, WINDOW), 1)
    return jnp.where(column - row == offset, 1.0, 0.0).astype(jnp.bfloat16)


def place(offset, window):
    moved = jnp.dot(selector(offset), window, preferred_element_type=jnp.float32)
    return moved.astype(window.dtype)


def edges_kernel(offsets_ref, embed_ref, head_ref, lead_ref, trail_ref, sems):
    rank = lax.axis_index("tensor")
    copies = []
    for m, buffer in enumerate((embed_ref, head_ref)):
        begin = floor_tile(
            tail_begin(offsets_ref[m, rank], rank, buffer.shape[0], lead_ref.shape[1])
        )
        begin = pl.multiple_of(begin, TILE)
        copies.append(
            pltpu.make_async_copy(buffer.at[pl.ds(0, lead_ref.shape[1])], lead_ref.at[m], sems.at[2 * m])
        )
        copies.append(
            pltpu.make_async_copy(
                buffer.at[pl.ds(begin, trail_ref.shape[1])], trail_ref.at[m], sems.at[2 * m + 1]
            )
        )
    for copy in copies:
        copy.start()
    for copy in copies:
        copy.wait()


def pack_kernel(per_rank, per_step, picked_ref, meta_ref, embed_ref, head_ref, out_ref, rows, sems):
    height = embed_ref.shape[0]
    step = pl.program_id(0)

    @pl.when(step == 0)
    def _():
        copies = [
            pltpu.make_async_copy(buffer, rows.at[pl.ds(m * height, height)], sems.at[m])
            for m, buffer in enumerate((embed_ref, head_ref))
        ]
        for copy in copies:
            copy.start()
        for copy in copies:
            copy.wait()

    for q in range(per_step):
        block = picked_ref[step * per_step + q]
        m = (block >= per_rank).astype(jnp.int32)
        start = (block - m * per_rank) * BLOCK - meta_ref[m, 0]
        base = jnp.clip(floor_tile(start), 0, height - WINDOW)
        window = rows[pl.ds(pl.multiple_of(m * height + base, TILE), WINDOW), :]
        out_ref[q] = place(start - base, window)


def fix_kernel(per_rank, group, slots_ref, count_ref, picked_ref, meta_ref, packed_ref, left_ref, right_ref,
               out_ref, work, sems):
    count = count_ref[0]
    total = out_ref.shape[0]

    def keep(k):
        return pltpu.make_async_copy(packed_ref.at[slots_ref[k]], out_ref.at[slots_ref[k]], sems.at[k])

    def put(k):
        return pltpu.make_async_copy(work.at[k], out_ref.at[slots_ref[k]], sems.at[k])

    def start_keep(k, carry):
        keep(k).start()
        return carry

    def wait_keep(k, carry):
        keep(k).wait()
        return carry

    def start_put(k, carry):
        put(k).start()
        return carry

    def wait_put(k, carry):
        put(k).wait()
        return carry

    lax.fori_loop(count, total, start_keep, 0)
    row = lax.broadcasted_iota(jnp.int32, (BLOCK, work.shape[2]), 0)

    def one_group(g, carry):
        for q in range(group):
            k = g * group + q
            block = picked_ref[slots_ref[k]]
            m = (block >= per_rank).astype(jnp.int32)
            first = (block - m * per_rank) * BLOCK
            before, after, skew = meta_ref[m, 0], meta_ref[m, 1], meta_ref[m, 2]
            is_left = first < before
            left_base = jnp.clip(floor_tile(first + skew), 0, left_ref.shape[1] - WINDOW)
            right_base = jnp.clip(floor_tile(first - after), 0, right_ref.shape[1] - WINDOW)
            window = jnp.where(
                is_left,
                left_ref[m, pl.ds(pl.multiple_of(left_base, TILE), WINDOW), :],
                right_ref[m, pl.ds(pl.multiple_of(right_base, TILE), WINDOW), :],
            )
            offset = jnp.where(is_left, first + skew - left_base, first - after - right_base)
            low = jnp.where(is_left, 0, after - first)
            high = jnp.where(is_left, before - first, BLOCK)
            moved = jnp.dot(selector(offset), window, preferred_element_type=jnp.float32)
            kept = packed_ref[slots_ref[k]].astype(jnp.float32)
            work[k] = jnp.where((row >= low) & (row < high), moved, kept).astype(work.dtype)
        lax.fori_loop(g * group, jnp.minimum(count, (g + 1) * group), start_put, 0)
        return carry

    lax.fori_loop(0, (count + group - 1) // group, one_group, 0)
    lax.fori_loop(0, count, wait_put, 0)
    lax.fori_loop(count, total, wait_keep, 0)


def finish_kernel(n_data, per_step, position_ref, incoming_ref, probe_ref, stored_ref, sketch_ref):
    width = incoming_ref.shape[2]
    step = pl.program_id(0)
    for q in range(per_step):
        for d in range(n_data):
            where = position_ref[(step * per_step + q) * n_data + d]
            stored_ref[q, :, d * width : (d + 1) * width] = incoming_ref[where]
    rows = stored_ref[...].reshape(per_step * BLOCK, n_data * width)
    product = jnp.dot(rows, probe_ref[...], preferred_element_type=jnp.float32)
    sketch_ref[...] = product.reshape(sketch_ref.shape)


def edges(row_offsets, embed_rows, head_rows, quarter):
    width = embed_rows.shape[1]
    kind = embed_rows.dtype
    whole = pl.BlockSpec(memory_space=pltpu.VMEM)
    return pl.pallas_call(
        edges_kernel,
        grid_spec=pltpu.PrefetchScalarGridSpec(
            num_scalar_prefetch=1,
            grid=(),
            in_specs=[pl.BlockSpec(memory_space=pl.ANY)] * 2,
            out_specs=[whole, whole],
            scratch_shapes=[pltpu.SemaphoreType.DMA((4,))],
        ),
        out_shape=[
            jax.ShapeDtypeStruct((2, quarter, width), kind),
            jax.ShapeDtypeStruct((2, quarter + TILE, width), kind),
        ],
        name="edges",
    )(row_offsets, embed_rows, head_rows)


def pack(picked, meta, embed_rows, head_rows):
    height, width = embed_rows.shape
    count = picked.shape[0]
    per_step = 16
    kind = embed_rows.dtype
    return pl.pallas_call(
        functools.partial(pack_kernel, R // BLOCK, per_step),
        grid_spec=pltpu.PrefetchScalarGridSpec(
            num_scalar_prefetch=2,
            grid=(count // per_step,),
            in_specs=[pl.BlockSpec(memory_space=pl.ANY)] * 2,
            out_specs=pl.BlockSpec((per_step, BLOCK, width), lambda i, *_: (i, 0, 0)),
            scratch_shapes=[
                pltpu.VMEM((2 * height, width), kind),
                pltpu.SemaphoreType.DMA((2,)),
            ],
        ),
        out_shape=jax.ShapeDtypeStruct((count, BLOCK, width), kind),
        compiler_params=pltpu.CompilerParams(
            dimension_semantics=("arbitrary",), vmem_limit_bytes=24 * MIB
        ),
        cost_estimate=pl.CostEstimate(
            flops=2 * count * BLOCK * WINDOW * width, bytes_accessed=24 * MIB, transcendentals=0
        ),
        name="pack",
    )(picked, meta, embed_rows, head_rows)


def fix(slots, count, picked, meta, packed, from_left, from_right):
    most, group = 4 * (R // 4) // BLOCK, 8
    return pl.pallas_call(
        functools.partial(fix_kernel, R // BLOCK, group),
        grid_spec=pltpu.PrefetchScalarGridSpec(
            num_scalar_prefetch=4,
            grid=(),
            in_specs=[
                pl.BlockSpec(memory_space=pltpu.VMEM),
                pl.BlockSpec(memory_space=pltpu.VMEM),
                pl.BlockSpec(memory_space=pltpu.VMEM),
            ],
            out_specs=pl.BlockSpec(memory_space=pl.ANY),
            scratch_shapes=[
                pltpu.VMEM((most,) + packed.shape[1:], packed.dtype),
                pltpu.SemaphoreType.DMA((packed.shape[0],)),
            ],
        ),
        out_shape=jax.ShapeDtypeStruct(packed.shape, packed.dtype),
        compiler_params=pltpu.CompilerParams(vmem_limit_bytes=57 * MIB),
        name="fix",
    )(slots, count, picked, meta, packed, from_left, from_right)


def finish(position, incoming, probe, slot_count, n_data):
    columns, sketch_width = probe.shape
    per_step = 4
    return pl.pallas_call(
        functools.partial(finish_kernel, n_data, per_step),
        grid_spec=pltpu.PrefetchScalarGridSpec(
            num_scalar_prefetch=1,
            grid=(slot_count // per_step,),
            in_specs=[
                pl.BlockSpec(incoming.shape, lambda i, *_: (0, 0, 0)),
                pl.BlockSpec(probe.shape, lambda i, *_: (0, 0)),
            ],
            out_specs=[
                pl.BlockSpec((per_step, BLOCK, columns), lambda i, *_: (i, 0, 0)),
                pl.BlockSpec((per_step, BLOCK, sketch_width), lambda i, *_: (i, 0, 0)),
            ],
        ),
        out_shape=[
            jax.ShapeDtypeStruct((slot_count, BLOCK, columns), incoming.dtype),
            jax.ShapeDtypeStruct((slot_count, BLOCK, sketch_width), jnp.float32),
        ],
        compiler_params=pltpu.CompilerParams(
            dimension_semantics=("arbitrary",), vmem_limit_bytes=48 * MIB
        ),
        name="finish",
    )(position, incoming, probe)


def shards(embed_rows, head_rows, row_offsets, slot_table, probe):
    n_tensor = lax.axis_size("tensor")
    n_data = lax.axis_size("dp")
    my_tensor = lax.axis_index("tensor")
    my_data = lax.axis_index("dp")
    quarter = R // 4
    height = embed_rows.shape[0]

    lead_part, trail_part = edges(row_offsets, embed_rows, head_rows, quarter)
    from_left = from_behind(trail_part, "tensor", 1)
    from_right = from_behind(lead_part, "tensor", -1)
    left = (my_tensor + n_tensor - 1) % n_tensor
    left_begin = tail_begin(row_offsets[:, left], left, height, quarter)
    skew = left_begin - floor_tile(left_begin)
    meta = jnp.stack(
        [row_offsets[:, my_tensor] - my_tensor * R, row_offsets[:, my_tensor + 1] - my_tensor * R, skew], axis=1
    )

    devices = n_tensor * n_data
    per_rank = R // BLOCK
    total_blocks = per_rank * n_tensor
    slot_count = 2 * total_blocks // devices
    max_from = slot_count // n_tensor
    slot_grid = slot_table.reshape(devices, slot_count)
    source = slot_grid % total_blocks // per_rank
    local_block = slot_grid // total_blocks * per_rank + slot_grid % per_rank
    from_me = source == my_tensor
    slot_range = jnp.arange(slot_count, dtype=jnp.int32)
    lower = slot_range[None, :] < slot_range[:, None]
    rank_order = jnp.sum((from_me[:, None, :] & lower[None]).astype(jnp.int32), axis=2)
    slot_index = jnp.arange(max_from, dtype=jnp.int32)
    select = from_me[:, None, :] & (rank_order[:, None, :] == slot_index[None, :, None])
    picked = jnp.sum(jnp.where(select, local_block[:, None, :], 0), axis=2).reshape(-1)
    writer = my_data * n_tensor + my_tensor
    my_source = source[writer]
    earlier = (my_source[None, :] == my_source[:, None]) & lower
    rank_within = jnp.sum(earlier.astype(jnp.int32), axis=1)
    data_range = jnp.arange(n_data, dtype=jnp.int32)
    position = (
        (data_range[None, :] * n_tensor + my_source[:, None]) * max_from + rank_within[:, None]
    ).reshape(-1)

    matrix = picked // per_rank
    first = picked % per_rank * BLOCK
    before = jnp.where(matrix == 0, meta[0, 0], meta[1, 0])
    after = jnp.where(matrix == 0, meta[0, 1], meta[1, 1])
    on_edge = (first < before) | (first + BLOCK > after)
    everything = jnp.arange(picked.shape[0], dtype=jnp.int32)
    ahead = jnp.sum((on_edge[None, :] & (everything[None, :] < everything[:, None])).astype(jnp.int32), axis=1)
    count = jnp.sum(on_edge.astype(jnp.int32)).reshape(1)
    turn = jnp.where(on_edge, ahead, count + everything - ahead)
    slots = jnp.sum(jnp.where(turn[None, :] == everything[:, None], everything[None, :], 0), axis=1)

    packed = pack(picked, meta, embed_rows, head_rows)
    outgoing = fix(slots, count, picked, meta, packed, from_left, from_right)
    incoming = lax.all_to_all(outgoing, ("dp", "tensor"), split_axis=0, concat_axis=0, tiled=True)
    stored, sketch = finish(position, incoming, probe, slot_count, n_data)
    return (stored, sketch)


def solution(mesh):
    return jax.shard_map(
        shards,
        mesh=mesh,
        in_specs=(P("tensor", "dp"), P("tensor", "dp"), P(), P(), P()),
        out_specs=(P(("dp", "tensor"), None, None), P(("dp", "tensor"), None, None)),
        check_vma=False,
    )
```

profile of v0, /device:TPU:0, one launch (start us, length us, event | category | flops | bytes accessed | tf_op | source)
XLA Modules:
  0.0 152.0 jit_solution(3573465903058682021)
XLA Ops:
  0.6 0.0 copy-start.6
  0.6 0.0 copy-start.1
  0.6 0.0 copy-start.7
  0.7 3.8 %edges.1 = (bf16[2,2048,128]{2,1,0:T(8,128)(2,1)}, bf16[2,2064,128]{2,1,0:T(8,128)(2,1)}) custom-call(s32[2,9]{1,0:T(2,128)} %offsets_ref.1, bf16[12288,128]{1,0:T(8,128)(2,1)} %embed_ref.3, bf16[12288,128]{1,0:T(8,128)(2,1)} %head_ref.3), custom_call_target="tpu_custom_call" | custom-call | tf_op jit(solution)/shard_map/edges/pallas_call | solution.py:163
  4.5 3.4 %collective-permute-start.1 = (bf16[2,2048,128]{2,1,0:T(8,128)(2,1)}, bf16[2,2048,128]{2,1,0:T(8,128)(2,1)}, u32[]{:S(2)}, u32[]{:S(2)}) collective-permute-start(bf16[2,2048,128]{2,1,0:T(8,128)(2,1)} %get-tuple-element.5), channel_id=1, source_target_pairs={{1,0},{2,1},{3,2},{4,3},{5,4},{6,5},{7,6},{0,7},{9,8},{10,9},{11,1... | collective-permute-start | bytes 3145736 | tf_op jit(solution)/shard_map/ppermute | solution.py:20
  7.9 0.0 collective-permute-start
  7.9 0.0 copy-done.7
  7.9 0.1 reshape.228
  8.0 0.6 convert_reduce_fusion
  8.7 0.1 select_reduce_fusion.1
  8.8 0.0 copy-done.6
  8.8 0.1 shift-left_subtract_fusion
  8.9 0.1 pad_add_fusion.meta_ref
  9.0 0.0 copy-start.5
  9.0 0.1 copy.7
  9.1 0.1 reshape.229.picked_ref
  9.2 0.0 copy-done.1
  9.2 0.0 copy-start.2
  9.2 1.9 %copy-done.2 = bf16[12288,128]{1,0:T(8,128)(2,1)S(1)} copy-done((bf16[12288,128]{1,0:T(8,128)(2,1)S(1)}, bf16[12288,128]{1,0:T(8,128)(2,1)}, u32[]{:S(2)}) %copy-start.2) | copy-done | bytes 3145752
  11.1 0.0 copy-start.4
  11.1 4.6 %pack.1.packed_ref = bf16[128,128,128]{2,1,0:T(8,128)(2,1)S(1)} custom-call(s32[128]{0:T(128)S(1)} %reshape.229.picked_ref, s32[2,3]{1,0:T(2,128)S(1)} %pad_add_fusion.meta_ref, bf16[12288,128]{1,0:T(8,128)(2,1)S(1)} %copy-done.1, bf16[12288,128]{1,0:T(8,128)(2,1)S(1)} %copy-done.2), custom_call_target="tpu_custom_call" | custom-call | flops 1073741824 | bytes 25165824 | tf_op jit(solution)/shard_map/pack/pallas_call | solution.py:185
  15.7 0.0 copy-done.5
  15.7 0.0 copy-start
  15.7 2.0 %copy-done = bf16[128,128,128]{2,1,0:T(8,128)(2,1)} copy-done((bf16[128,128,128]{2,1,0:T(8,128)(2,1)}, bf16[128,128,128]{2,1,0:T(8,128)(2,1)S(1)}, u32[]{:S(2)}) %copy-start) | copy-done | bytes 4194328
  17.7 0.6 fusion.15
  18.3 3.1 %convert_reduce_fusion.3 = s32[]{:T(128)} fusion(s32[32,4]{0,1:T(4,128)S(1)} %select_reduce_fusion.1, s32[]{:T(128)} %bitcast.4, s32[]{:T(128)} %bitcast.3, s32[]{:T(128)} %bitcast.2, s32[]{:T(128)} %bitcast.1), kind=kLoop, calls=%fused_computation.40 | loop fusion | flops 3711 | bytes 532 | tf_op jit(solution)/shard_map/reduce_sum | solution.py:309
  21.4 2.5 %compare_or_fusion = pred[128]{0:T(512)(128)(4,1)S(1)} fusion(s32[128]{0:T(128)S(1)} %reshape.229.picked_ref, s32[]{:T(128)} %bitcast.4, s32[]{:T(128)} %bitcast.3, s32[]{:T(128)} %bitcast.2, s32[]{:T(128)} %bitcast.1), kind=kLoop, calls=%fused_computation.46 | loop fusion | flops 3456 | bytes 656 | tf_op jit(solution)/shard_map/or | solution.py:306
  23.9 0.1 convert_reduce_fusion.1
  24.0 0.0 copy-done.4
  24.0 3.0 %subtract_select_fusion = s32[128]{0:T(128)S(1)} fusion(s32[128]{0:T(128)S(1)} %convert_reduce_fusion.1, s32[]{:T(128)} %convert_reduce_fusion.3, s32[]{:T(128)} %bitcast.4, s32[]{:T(128)} %bitcast.3, s32[]{:T(128)} %bitcast.2, s32[]{:T(128)} %bitcast.1, s32[128]{0:T(128)S(1)} %reshape.229.picked_ref), kind=kLoop, calls=%fused_computation.59 | loop fusion | flops 3840 | bytes 1556 | tf_op jit(solution)/shard_map/jit(_where)/select_n | solution.py:310
  27.0 0.6 select_reduce_fusion.slots_ref
  27.6 3.3 %collective-permute-done.1.right_ref = bf16[2,2048,128]{2,1,0:T(8,128)(2,1)} collective-permute-done((bf16[2,2048,128]{2,1,0:T(8,128)(2,1)}, bf16[2,2048,128]{2,1,0:T(8,128)(2,1)}, u32[]{:S(2)}, u32[]{:S(2)}) %collective-permute-start.1) | collective-permute-done | bytes 1048608 | tf_op jit(solution)/shard_map/ppermute | solution.py:20
  31.0 1.9 %collective-permute-done.left_ref = bf16[2,2064,128]{2,1,0:T(8,128)(2,1)} collective-permute-done((bf16[2,2064,128]{2,1,0:T(8,128)(2,1)}, bf16[2,2064,128]{2,1,0:T(8,128)(2,1)}, u32[]{:S(2)}, u32[]{:S(2)}) %collective-permute-start) | collective-permute-done | bytes 1056800 | tf_op jit(solution)/shard_map/ppermute | solution.py:20
  32.9 8.0 %fix.1 = bf16[128,128,128]{2,1,0:T(8,128)(2,1)} custom-call(s32[128]{0:T(128)} %select_reduce_fusion.slots_ref, s32[1]{0:T(128)} %bitcast.5.count_ref, s32[128]{0:T(128)} %copy-done.4, s32[2,3]{1,0:T(2,128)} %copy-done.5, bf16[128,128,128]{2,1,0:T(8,128)(2,1)} %copy-done, bf16[2,2064,128]{2,1,0:T(8,128)(2,1)} %collective-permute-done.left_ref, ...), custom_call_target="tpu_custom_call" | custom-call | tf_op jit(solution)/shard_map/fix/pallas_call | solution.py:210
  40.8 0.0 copy-start.3
  40.8 5.6 %all-to-all-start = ((bf16[128,128,128]{2,1,0:T(8,128)(2,1)}), bf16[128,128,128]{2,1,0:T(8,128)(2,1)}, u32[]{:S(2)}, u32[]{:S(2)}) async-start(bf16[128,128,128]{2,1,0:T(8,128)(2,1)} %fix.1), calls=%async_computation | async-start | bytes 8388608 | tf_op jit(solution)/shard_map/all_to_all | solution.py:315
  46.5 0.2 convert_reduce_fusion.2
  46.7 0.1 multiply_add_fusion
  46.8 0.1 add.154.position_ref
  46.9 93.3 %all-to-all-done.incoming_ref = bf16[128,128,128]{2,1,0:T(8,128)(2,1)} async-done(((bf16[128,128,128]{2,1,0:T(8,128)(2,1)}), bf16[128,128,128]{2,1,0:T(8,128)(2,1)}, u32[]{:S(2)}, u32[]{:S(2)}) %all-to-all-start) | async-done | bytes 4194336 | tf_op jit(solution)/shard_map/all_to_all | solution.py:315
  140.2 0.0 copy-done.3
  140.2 11.8 %finish.1 = (bf16[32,128,512]{2,1,0:T(8,128)(2,1)}, f32[32,128,1024]{2,1,0:T(8,128)}) custom-call(s32[128]{0:T(128)S(1)} %add.154.position_ref, bf16[128,128,128]{2,1,0:T(8,128)(2,1)} %all-to-all-done.incoming_ref, bf16[512,1024]{1,0:T(8,128)(2,1)S(1)} %copy-done.3), custom_call_target="tpu_custom_call" | custom-call | tf_op jit(solution)/shard_map/finish/pallas_call | solution.py:235
  (4 shorter events, 0.1 us)
Async XLA Ops:
  0.6 8.2 %copy-start.6 = (s32[2,9]{1,0:T(2,128)S(1)}, s32[2,9]{1,0:T(2,128)}, u32[]{:S(2)}) copy-start(s32[2,9]{1,0:T(2,128)} %offsets_ref.1) | copy-start | bytes 220
  0.6 8.6 %copy-start.1 = (bf16[12288,128]{1,0:T(8,128)(2,1)S(1)}, bf16[12288,128]{1,0:T(8,128)(2,1)}, u32[]{:S(2)}) copy-start(bf16[12288,128]{1,0:T(8,128)(2,1)} %embed_ref.3) | copy-start | bytes 9437188
  0.6 7.3 %copy-start.7 = (s32[1024]{0:T(1024)S(1)}, s32[1024]{0:T(1024)}, u32[]{:S(2)}) copy-start(s32[1024]{0:T(1024)} %param.8) | copy-start | bytes 12292
  4.5 26.5 %collective-permute-start.1 = (bf16[2,2048,128]{2,1,0:T(8,128)(2,1)}, bf16[2,2048,128]{2,1,0:T(8,128)(2,1)}, u32[]{:S(2)}, u32[]{:S(2)}) collective-permute-start(bf16[2,2048,128]{2,1,0:T(8,128)(2,1)} %get-tuple-element.5), channel_id=1, source_target_pairs={{1,0},{2,1},{3,2},{4,3},{5,4},{6,5},{7,6},{0,7},{9,8},{10,9},{11,1... | collective-permute-start | bytes 3145736 | tf_op jit(solution)/shard_map/ppermute | solution.py:20
  7.9 25.0 %collective-permute-start = (bf16[2,2064,128]{2,1,0:T(8,128)(2,1)}, bf16[2,2064,128]{2,1,0:T(8,128)(2,1)}, u32[]{:S(2)}, u32[]{:S(2)}) collective-permute-start(bf16[2,2064,128]{2,1,0:T(8,128)(2,1)} %get-tuple-element.4), channel_id=1, source_target_pairs={{7,0},{0,1},{1,2},{2,3},{3,4},{4,5},{5,6},{6,7},{15,8},{8,9},{9,10... | collective-permute-start | bytes 3170312 | tf_op jit(solution)/shard_map/ppermute | solution.py:20
  9.0 6.7 %copy-start.5 = (s32[2,3]{1,0:T(2,128)}, s32[2,3]{1,0:T(2,128)S(1)}, u32[]{:S(2)}) copy-start(s32[2,3]{1,0:T(2,128)S(1)} %pad_add_fusion.meta_ref) | copy-start | bytes 76
  9.2 1.9 %copy-start.2 = (bf16[12288,128]{1,0:T(8,128)(2,1)S(1)}, bf16[12288,128]{1,0:T(8,128)(2,1)}, u32[]{:S(2)}) copy-start(bf16[12288,128]{1,0:T(8,128)(2,1)} %head_ref.3) | copy-start | bytes 9437188
  11.1 12.9 %copy-start.4 = (s32[128]{0:T(128)}, s32[128]{0:T(128)S(1)}, u32[]{:S(2)}) copy-start(s32[128]{0:T(128)S(1)} %reshape.229.picked_ref) | copy-start | bytes 1540
  15.7 2.0 %copy-start = (bf16[128,128,128]{2,1,0:T(8,128)(2,1)}, bf16[128,128,128]{2,1,0:T(8,128)(2,1)S(1)}, u32[]{:S(2)}) copy-start(bf16[128,128,128]{2,1,0:T(8,128)(2,1)S(1)} %pack.1.packed_ref) | copy-start | bytes 12582916
  40.8 99.3 %copy-start.3 = (bf16[512,1024]{1,0:T(8,128)(2,1)S(1)}, bf16[512,1024]{1,0:T(8,128)(2,1)}, u32[]{:S(2)}) copy-start(bf16[512,1024]{1,0:T(8,128)(2,1)} %probe_ref.1) | copy-start | bytes 3145732
  40.8 99.3 %all-to-all-start = ((bf16[128,128,128]{2,1,0:T(8,128)(2,1)}), bf16[128,128,128]{2,1,0:T(8,128)(2,1)}, u32[]{:S(2)}, u32[]{:S(2)}) async-start(bf16[128,128,128]{2,1,0:T(8,128)(2,1)} %fix.1), calls=%async_computation | async-start | bytes 8388608 | tf_op jit(solution)/shard_map/all_to_all | solution.py:315
where the time goes:
time: 153 us; the launch traced here: 152 us
  waiting for transfers between devices  98.5 us (64%)
  Pallas kernels  28.1 us (18%)
  other arithmetic  10.5 us (7%)
  starting transfers between devices  9.04 us (6%)
  local copies, waits for them, and re-layouts  4.9 us (3%)
    all_to_all x1, waiting for transfers between devices, shards(): lax.all_to_all(outgoing, ('dp', 'tensor'), split_axis=0, concat_axis=0, t...  93.3 us
    pallas_call x1, Pallas kernels, finish(): pl.pallas_call(functools.partial(finish_kernel, n_data, per_step), grid_s...  11.8 us
    pallas_call x1, Pallas kernels, fix(): pl.pallas_call(functools.partial(fix_kernel, R // BLOCK, group), grid_spe...  7.95 us
    all_to_all x1, starting transfers between devices, shards(): lax.all_to_all(outgoing, ('dp', 'tensor'), split_axis=0, concat_axis=0, t...  5.63 us
    ppermute x2, waiting for transfers between devices, from_behind(): return lax.ppermute(block, axis, route)  5.24 us
    pallas_call x1, Pallas kernels, pack(): pl.pallas_call(functools.partial(pack_kernel, R // BLOCK, per_step), grid...  4.6 us
    unnamed x16, local copies, waits for them, and re-layouts  3.92 us
    pallas_call x1, Pallas kernels, edges(): pl.pallas_call(edges_kernel, grid_spec=pltpu.PrefetchScalarGridSpec(num_s...  3.82 us
  transfers between devices with their start and end apart: 3, of which 3 were waited for; matrix products, arithmetic and copies ran while one was open for 8% of the time, Pallas kernels for 3%

commit v1 on v0

v1 whole, which is shorter than its diff:
```python
import functools

import jax
import jax.numpy as jnp
from jax import lax
from jax.experimental import pallas as pl
from jax.experimental.pallas import tpu as pltpu
from jax.sharding import PartitionSpec as P

MESH = pl.DeviceIdType.MESH
AXES = ("dp", "tensor")
BLOCK = 128
TILE = 16
WINDOW = 256
MIB = 1 << 20


def tile_of(value):
    return lax.shift_right_arithmetic(value, 4)


def tail_begin(offset, rank, span, height):
    return jnp.clip((rank + 1) * span - offset, 0, height - span // 4 - 1)


def selector(offset):
    row = lax.broadcasted_iota(jnp.int32, (BLOCK, WINDOW), 0)
    column = lax.broadcasted_iota(jnp.int32, (BLOCK, WINDOW), 1)
    return jnp.where(column - row == offset, 1.0, 0.0).astype(jnp.bfloat16)


def moved(offset, window):
    return jnp.dot(selector(offset), window, preferred_element_type=jnp.float32)


def plan_kernel(n_tensor, per_rank, first_turns, offsets_ref, grid_ref, picks_ref, where_ref, late_ref):
    me = lax.axis_index("tensor")
    span = per_rank * BLOCK
    grid = grid_ref[...]
    devices, slots = grid.shape
    total = n_tensor * per_rank
    matrix = (grid >= total).astype(jnp.int32)
    within = grid - matrix * total
    source = lax.shift_right_logical(within, per_rank.bit_length() - 1)
    block = within - source * per_rank
    first = block * BLOCK
    far = jnp.zeros(grid.shape, jnp.int32)
    for m in range(2):
        for t in range(n_tensor):
            if t % 2 == 0:
                touched = first < offsets_ref[m, t] - t * span
            else:
                touched = first + BLOCK > offsets_ref[m, t + 1] - t * span
            here = (source == t) & (matrix == m)
            far = far + jnp.where(here & touched, 1, 0)
    lane = lax.broadcasted_iota(jnp.int32, grid.shape, 1)
    key = far * slots + lane
    turn = jnp.zeros(grid.shape, jnp.int32)
    for s in range(slots):
        ahead = (source[:, s : s + 1] == source) & (key[:, s : s + 1] < key)
        turn = turn + jnp.where(ahead, 1, 0)
    most = slots // n_tensor
    local = matrix * per_rank + block
    column = lax.broadcasted_iota(jnp.int32, picks_ref.shape, 1)
    picks = jnp.zeros(picks_ref.shape, jnp.int32)
    for j in range(most):
        chosen = jnp.where((source == me) & (turn == j), local, 0)
        picks = jnp.where(column == j, jnp.sum(chosen, axis=1, keepdims=True), picks)
    picks_ref[...] = picks
    where_ref[...] = source * most + turn
    wrong = jnp.where(turn < first_turns, far, 0)
    late_ref[...] = jnp.sum(jnp.sum(wrong, axis=1, keepdims=True), axis=0, keepdims=True)


def exchange_kernel(n_data, n_tensor, per_rank, first_turns, picks_ref, offsets_ref, embed_ref, head_ref,
                    incoming_ref, again_ref, rows, trail, near, far, ready, rest,
                    load_sems, edge_send, edge_recv, send_sems, recv_sems):
    data, rank = lax.axis_index("dp"), lax.axis_index("tensor")
    devices = n_data * n_tensor
    me = data * n_tensor + rank
    span = per_rank * BLOCK
    height = rows.shape[1] * TILE
    edge = trail.shape[1]
    most = incoming_ref.shape[0] // devices
    last_turns = most - first_turns
    even = rank % 2 == 0
    near_rank = jnp.where(even, rank + 1, rank - 1)
    far_rank = jnp.where(even, (rank + n_tensor - 1) % n_tensor, (rank + 1) % n_tensor)
    left = (rank + n_tensor - 1) % n_tensor

    loads = [
        pltpu.make_async_copy(buffer, rows.at[m], load_sems.at[m])
        for m, buffer in enumerate((embed_ref, head_ref))
    ]
    for load in loads:
        load.start()

    def peer(k):
        return (data + k % n_data) % n_data, (rank + k // n_data) % n_tensor

    barrier = pltpu.get_barrier_semaphore()

    def greet(k, carry):
        d, t = peer(k)
        pl.semaphore_signal(barrier, inc=1, device_id=(d, t), device_id_type=MESH)
        return carry

    lax.fori_loop(1, devices, greet, 0)

    for load in loads:
        load.wait()

    def fill(i, carry):
        for m in range(2):
            trail[m, i] = rows[m, tile_of(tail_begin(offsets_ref[m, rank], rank, span, height)) + i]
        return carry

    lax.fori_loop(0, edge, fill, 0)
    pl.semaphore_wait(barrier, devices - 1)

    lead = rows.at[:, pl.ds(0, edge)]

    def edge_copy(source, target, which, t):
        return pltpu.make_async_remote_copy(
            src_ref=source, dst_ref=target, send_sem=edge_send.at[which], recv_sem=edge_recv.at[which],
            device_id=(data, t), device_id_type=MESH,
        )

    @pl.when(even)
    def _():
        edge_copy(trail, near, 0, near_rank).start()
        edge_copy(lead, far, 1, far_rank).start()

    @pl.when(jnp.logical_not(even))
    def _():
        edge_copy(lead, near, 0, near_rank).start()
        edge_copy(trail, far, 1, far_rank).start()

    row = lax.broadcasted_iota(jnp.int32, (BLOCK, rows.shape[3]), 0)

    def window(buffer, m, start):
        base = jnp.clip(tile_of(start), 0, buffer.shape[1] - WINDOW // TILE)
        tiles = [buffer[m, base + i] for i in range(WINDOW // TILE)]
        return jnp.concatenate(tiles, axis=0), start - base * TILE

    def gathered(dest, j, with_far):
        number = picks_ref[dest, j]
        m = (number >= per_rank).astype(jnp.int32)
        first = (number - m * per_rank) * BLOCK
        low = jnp.where(m == 0, offsets_ref[0, rank], offsets_ref[1, rank]) - rank * span - first
        high = jnp.where(m == 0, offsets_ref[0, rank + 1], offsets_ref[1, rank + 1]) - rank * span - first
        left_begin = tail_begin(jnp.where(m == 0, offsets_ref[0, left], offsets_ref[1, left]), left, span, height)
        own, own_offset = window(rows, m, -low)
        from_left = first + left_begin - tile_of(left_begin) * TILE
        from_right = -high
        piece, offset = window(near, m, jnp.where(even, from_right, from_left))
        if with_far:
            use_far = jnp.where(even, low > 0, high < BLOCK)
            other, other_offset = window(far, m, jnp.where(even, from_left, from_right))
            piece = jnp.where(use_far, other, piece)
            offset = jnp.where(use_far, other_offset, offset)
        kept = moved(own_offset, own)
        patch = moved(offset, piece)
        return jnp.where((row >= low) & (row < high), kept, patch).astype(rows.dtype)

    def send(phase, staged, count, base, d, t):
        to = d * n_tensor + t
        return pltpu.make_async_remote_copy(
            src_ref=staged.at[pl.ds(to * count, count)],
            dst_ref=incoming_ref.at[pl.ds(me * most + base, count)],
            send_sem=send_sems.at[phase, to], recv_sem=recv_sems.at[phase, me],
            device_id=(d, t), device_id_type=MESH,
        )

    def wait_edge(which, target):
        copy = edge_copy(trail, target, which, near_rank)
        copy.wait_recv()

    def phase_of(phase, staged, count, base, with_far):
        for j in range(count):
            incoming_ref[me * most + base + j] = gathered(me, base + j, with_far)

        def one(k, carry):
            d, t = peer(k)
            to = d * n_tensor + t
            for j in range(count):
                staged[to * count + j] = gathered(to, base + j, with_far)

            @pl.when(k > 1)
            def _():
                send(phase, staged, count, base, *peer(k - 1)).start()

            return carry

        lax.fori_loop(1, devices, one, 0)
        send(phase, staged, count, base, *peer(devices - 1)).start()

    wait_edge(0, near)
    if first_turns:
        phase_of(0, ready, first_turns, 0, False)
    wait_edge(1, far)
    phase_of(1, rest, last_turns, first_turns, True)

    if first_turns:
        def redo(to, carry):
            for j in range(first_turns):
                again_ref[to * first_turns + j] = gathered(to, j, True)
            return carry

        lax.fori_loop(0, devices, redo, 0)
    else:
        again_ref[...] = jnp.zeros_like(again_ref)

    edge_copy(trail, near, 0, near_rank).wait_send()
    edge_copy(trail, far, 1, far_rank).wait_send()

    def finish_phase(phase, staged, count, base):
        def drain(k, carry):
            d, t = peer(k)
            send(phase, staged, count, base, d, t).wait_send()
            pltpu.make_async_remote_copy(
                src_ref=staged.at[pl.ds(me * count, count)],
                dst_ref=incoming_ref.at[pl.ds((d * n_tensor + t) * most + base, count)],
                send_sem=send_sems.at[phase, me], recv_sem=recv_sems.at[phase, d * n_tensor + t],
                device_id=(d, t), device_id_type=MESH,
            ).wait_recv()
            return carry

        lax.fori_loop(1, devices, drain, 0)

    if first_turns:
        finish_phase(0, ready, first_turns, 0)
    finish_phase(1, rest, last_turns, first_turns)


def finish_kernel(n_data, n_tensor, per_step, where_ref, incoming_ref, probe_ref, stored_ref, sketch_ref):
    width = incoming_ref.shape[2]
    stride = incoming_ref.shape[0] // n_data
    me = lax.axis_index("dp") * n_tensor + lax.axis_index("tensor")
    step = pl.program_id(0)
    for q in range(per_step):
        base = where_ref[me, step * per_step + q]
        for d in range(n_data):
            stored_ref[q, :, d * width : (d + 1) * width] = incoming_ref[base + d * stride]
    rows = stored_ref[...].reshape(per_step * BLOCK, n_data * width)
    product = jnp.dot(rows, probe_ref[...], preferred_element_type=jnp.float32)
    sketch_ref[...] = product.reshape(sketch_ref.shape)


def plan(row_offsets, slot_grid, n_tensor, per_rank, first_turns):
    devices, slots = slot_grid.shape
    vmem = pl.BlockSpec(memory_space=pltpu.VMEM)
    return pl.pallas_call(
        functools.partial(plan_kernel, n_tensor, per_rank, first_turns),
        in_specs=[pl.BlockSpec(memory_space=pltpu.SMEM), vmem],
        out_specs=[vmem, vmem, vmem],
        out_shape=[
            jax.ShapeDtypeStruct((devices, slots // n_tensor), jnp.int32),
            jax.ShapeDtypeStruct((devices, slots), jnp.int32),
            jax.ShapeDtypeStruct((1, 1), jnp.int32),
        ],
        name="plan",
    )(row_offsets, slot_grid)


def exchange(picks, row_offsets, embed_rows, head_rows, n_data, n_tensor, per_rank, first_turns):
    height, width = embed_rows.shape
    kind = embed_rows.dtype
    devices = n_data * n_tensor
    most = picks.shape[1]
    edge = per_rank * BLOCK // 4 // TILE + 1
    smem = pl.BlockSpec(memory_space=pltpu.SMEM)
    vmem = pl.BlockSpec(memory_space=pltpu.VMEM)
    hbm = pl.BlockSpec(memory_space=pltpu.HBM)
    return pl.pallas_call(
        functools.partial(exchange_kernel, n_data, n_tensor, per_rank, first_turns),
        in_specs=[smem, smem, hbm, hbm],
        out_specs=[vmem, vmem],
        out_shape=[
            jax.ShapeDtypeStruct((devices * most, BLOCK, width), kind),
            jax.ShapeDtypeStruct((devices * max(first_turns, 1), BLOCK, width), kind),
        ],
        scratch_shapes=[
            pltpu.VMEM((2, height // TILE, TILE, width), kind),
            pltpu.VMEM((2, edge, TILE, width), kind),
            pltpu.VMEM((2, edge, TILE, width), kind),
            pltpu.VMEM((2, edge, TILE, width), kind),
            pltpu.VMEM((devices * max(first_turns, 1), BLOCK, width), kind),
            pltpu.VMEM((devices * (most - first_turns), BLOCK, width), kind),
            pltpu.SemaphoreType.DMA((2,)),
            pltpu.SemaphoreType.DMA((2,)),
            pltpu.SemaphoreType.DMA((2,)),
            pltpu.SemaphoreType.DMA((2, devices)),
            pltpu.SemaphoreType.DMA((2, devices)),
        ],
        compiler_params=pltpu.CompilerParams(
            collective_id=0, has_side_effects=True, vmem_limit_bytes=32 * MIB
        ),
        name="exchange",
    )(picks, row_offsets, embed_rows.reshape(-1, TILE, width), head_rows.reshape(-1, TILE, width))


def finish(where, incoming, probe, n_data, n_tensor):
    columns, sketch_width = probe.shape
    slot_count = where.shape[1]
    per_step = 4
    return pl.pallas_call(
        functools.partial(finish_kernel, n_data, n_tensor, per_step),
        grid_spec=pltpu.PrefetchScalarGridSpec(
            num_scalar_prefetch=1,
            grid=(slot_count // per_step,),
            in_specs=[
                pl.BlockSpec(memory_space=pltpu.VMEM),
                pl.BlockSpec(memory_space=pltpu.VMEM),
            ],
            out_specs=[
                pl.BlockSpec((per_step, BLOCK, columns), lambda i, *_: (i, 0, 0)),
                pl.BlockSpec((per_step, BLOCK, sketch_width), lambda i, *_: (i, 0, 0)),
            ],
        ),
        out_shape=[
            jax.ShapeDtypeStruct((slot_count, BLOCK, columns), incoming.dtype),
            jax.ShapeDtypeStruct((slot_count, BLOCK, sketch_width), jnp.float32),
        ],
        compiler_params=pltpu.CompilerParams(
            dimension_semantics=("arbitrary",), vmem_limit_bytes=32 * MIB
        ),
        name="finish",
    )(where, incoming, probe)


def shards(embed_rows, head_rows, row_offsets, slot_table, probe):
    n_data, n_tensor = lax.axis_size("dp"), lax.axis_size("tensor")
    devices = n_data * n_tensor
    per_rank = slot_table.shape[0] // (2 * n_tensor)
    slots = slot_table.shape[0] // devices
    most = slots // n_tensor
    first_turns = most // 4
    picks, where, late = plan(row_offsets, slot_table.reshape(devices, slots), n_tensor, per_rank, first_turns)
    incoming, again = exchange(picks, row_offsets, embed_rows, head_rows, n_data, n_tensor, per_rank, first_turns)

    def ended(where, incoming, again, probe):
        return tuple(finish(where, incoming, probe, n_data, n_tensor))

    def resent(where, incoming, again, probe):
        fresh = lax.all_to_all(again, AXES, split_axis=0, concat_axis=0, tiled=True)
        shape = incoming.shape
        fresh = fresh.reshape((devices, first_turns) + shape[1:])
        held = incoming.reshape((devices, most) + shape[1:])
        whole = jnp.concatenate([fresh, held[:, first_turns:]], axis=1).reshape(shape)
        return ended(where, whole, again, probe)

    if not first_turns:
        return ended(where, incoming, again, probe)
    return lax.cond(late[0, 0] == 0, ended, resent, where, incoming, again, probe)


def solution(mesh):
    return jax.shard_map(
        shards,
        mesh=mesh,
        in_specs=(P("tensor", "dp"), P("tensor", "dp"), P(), P(), P()),
        out_specs=(P(AXES, None, None), P(AXES, None, None)),
        check_vma=False,
    )
```

time: 153 us -> 136 us (0.89)
  Pallas kernels: 28.1 us -> 128 us
  waiting for transfers between devices: 98.5 us -> 0 us
  other arithmetic: 10.5 us -> 0 us
  starting transfers between devices: 9.04 us -> 0 us
  local copies, waits for them, and re-layouts: 4.9 us -> 6.53 us
    pallas_call x4 -> x3, Pallas kernels: 28.1 us -> 128 us  [the longest x1 114 us: exchange(): pl.pallas_call(functools.partial(exchange_kernel, n_data, n_tensor, per_r...]
    all_to_all x1 -> x0, waiting for transfers between devices: 93.3 us -> none  [shards(): lax.all_to_all(outgoing, ('dp', 'tensor'), split_axis=0, concat_axis=0, t...]
    all_to_all x1 -> x0, starting transfers between devices: 5.63 us -> none  [shards(): lax.all_to_all(outgoing, ('dp', 'tensor'), split_axis=0, concat_axis=0, t...]
    ppermute x2 -> x0, waiting for transfers between devices: 5.24 us -> none  [from_behind(): return lax.ppermute(block, axis, route)]
    reduce_sum x6 -> x0, other arithmetic: 4.74 us -> none  [the longest x1 3.09 us: shards(): count = jnp.sum(on_edge.astype(jnp.int32)).reshape(1)]
    ppermute x2 -> x0, starting transfers between devices: 3.42 us -> none  [from_behind(): return lax.ppermute(block, axis, route)]
    select_n x1 -> x0, other arithmetic: 3.03 us -> none  [shards(): turn = jnp.where(on_edge, ahead, count + everything - ahead)]
    or x1 -> x0, other arithmetic: 2.46 us -> none  [shards(): on_edge = (first < before) | (first + BLOCK > after)]
  transfers between devices with their start and end apart: 3 -> 0, of which waited for: 3 -> 0; matrix products, arithmetic and copies ran while one was open for 8% -> 0% of each run, Pallas kernels for 3% -> 0%
where the time goes in v1:
time: 136 us
  Pallas kernels  128 us (94%)
  local copies, waits for them, and re-layouts  6.53 us (5%)
    pallas_call x1, Pallas kernels, exchange(): pl.pallas_call(functools.partial(exchange_kernel, n_data, n_tensor, per_r...  114 us
    pallas_call x1, Pallas kernels, finish(): pl.pallas_call(functools.partial(finish_kernel, n_data, n_tensor, per_ste...  12.3 us
    unnamed x8, local copies, waits for them, and re-layouts  5.17 us

profile of v1, /device:TPU:0, one launch (start us, length us, event | category | flops | bytes accessed | tf_op | source)
XLA Modules:
  0.0 136.0 jit_solution(15206157562220391423)
XLA Ops:
  0.6 1.4 %reshape.26.grid_ref = s32[32,32]{1,0:T(8,128)} reshape(s32[1024]{0:T(1024)} %param.10) | data formatting | bytes 8192 | tf_op jit(solution)/shard_map/reshape | solution.py:339
  2.0 1.9 %plan.1 = (s32[32,4]{1,0:T(8,128)}, s32[32,32]{1,0:T(8,128)S(1)}, s32[1,1]{1,0:T(1,128)}) custom-call(s32[2,9]{1,0:T(2,128)} %offsets_ref.3, s32[32,32]{1,0:T(8,128)} %reshape.26.grid_ref), custom_call_target="tpu_custom_call" | custom-call | tf_op jit(solution)/shard_map/plan/pallas_call | solution.py:253
  4.5 0.0 copy-start
  4.5 1.9 %copy-done = bf16[12288,128]{1,0:T(8,128)(2,1)S(1)} copy-done((bf16[12288,128]{1,0:T(8,128)(2,1)S(1)}, bf16[12288,128]{1,0:T(8,128)(2,1)}, u32[]{:S(2)}) %copy-start) | copy-done | bytes 3145752
  6.4 0.0 copy-start.1
  6.4 1.9 %copy-done.1 = bf16[12288,128]{1,0:T(8,128)(2,1)S(1)} copy-done((bf16[12288,128]{1,0:T(8,128)(2,1)S(1)}, bf16[12288,128]{1,0:T(8,128)(2,1)}, u32[]{:S(2)}) %copy-start.1) | copy-done | bytes 3145752
  8.3 0.0 copy-start.2
  8.3 0.7 copy-done.2
  9.0 0.0 copy-start.3
  9.0 0.7 copy-done.3
  9.7 113.9 %exchange.1 = (bf16[128,128,128]{2,1,0:T(8,128)(2,1)}, bf16[32,128,128]{2,1,0:T(8,128)(2,1)}) custom-call(s32[32,4]{1,0:T(8,128)S(1)} %copy-done.2, s32[2,9]{1,0:T(2,128)S(1)} %copy-done.3, bf16[768,16,128]{2,1,0:T(8,128)(2,1)S(1)} %bitcast.9, bf16[768,16,128]{2,1,0:T(8,128)(2,1)S(1)} %bitcast.10), custom_call_target="tpu_custom_call" | custom-call | tf_op jit(solution)/shard_map/exchange/pallas_call | solution.py:275
  123.6 12.4 %conditional.1 = ((bf16[32,128,512]{2,1,0:T(8,128)(2,1)}, f32[32,128,1024]{2,1,0:T(8,128)})) conditional(s32[]{:T(128)} %bitcast.5, (bf16[32,128,128]{2,1,0:T(8,128)(2,1)}, bf16[128,128,128]{2,1,0:T(8,128)(2,1)}, s32[32,32]{1,0:T(8,128)S(1)}, bf16[512,1024]{1,0:T(8,128)(2,1)}) %tuple.13, (s32[32,32]{1,0:T(8,128)S(1)}, ...), branch_computations={%region_0.0_spmd, %region_1.0_spmd} | conditional | flops 2097152 | bytes 22020164 | solution.py:355
  123.6 12.3 %finish.3 = (bf16[32,128,512]{2,1,0:T(8,128)(2,1)}, f32[32,128,1024]{2,1,0:T(8,128)}) custom-call(s32[32,32]{1,0:T(8,128)S(1)} %get-tuple-element.18.where_ref, bf16[128,128,128]{2,1,0:T(8,128)(2,1)} %get-tuple-element.19.incoming_ref, bf16[512,1024]{1,0:T(8,128)(2,1)} %get-tuple-element.20.probe_ref), custom_call_target="tpu_custom_call" | custom-call | tf_op jit(solution)/shard_map/cond/branch_1_fun/finish/pallas_call | solution.py:307
Async XLA Ops:
  4.5 1.9 %copy-start = (bf16[12288,128]{1,0:T(8,128)(2,1)S(1)}, bf16[12288,128]{1,0:T(8,128)(2,1)}, u32[]{:S(2)}) copy-start(bf16[12288,128]{1,0:T(8,128)(2,1)} %param.7) | copy-start | bytes 9437188
  6.4 1.9 %copy-start.1 = (bf16[12288,128]{1,0:T(8,128)(2,1)S(1)}, bf16[12288,128]{1,0:T(8,128)(2,1)}, u32[]{:S(2)}) copy-start(bf16[12288,128]{1,0:T(8,128)(2,1)} %param.8) | copy-start | bytes 9437188
  8.3 0.7 copy-start.2
  9.0 0.7 copy-start.3

commit v2 on v1

--- a/solution.py
+++ b/solution.py
@@ -12,6 +12,7 @@
 BLOCK = 128
 TILE = 16
 WINDOW = 256
+LANES = 128
 MIB = 1 << 20
 
 
@@ -33,11 +34,10 @@
     return jnp.dot(selector(offset), window, preferred_element_type=jnp.float32)
 
 
-def plan_kernel(n_tensor, per_rank, first_turns, offsets_ref, grid_ref, picks_ref, where_ref, late_ref):
+def plan_kernel(n_tensor, per_rank, slots, first_turns, offsets_ref, grid_ref, picks_ref, where_ref, late_ref):
     me = lax.axis_index("tensor")
     span = per_rank * BLOCK
     grid = grid_ref[...]
-    devices, slots = grid.shape
     total = n_tensor * per_rank
     matrix = (grid >= total).astype(jnp.int32)
     within = grid - matrix * total
@@ -54,27 +54,33 @@
             here = (source == t) & (matrix == m)
             far = far + jnp.where(here & touched, 1, 0)
     lane = lax.broadcasted_iota(jnp.int32, grid.shape, 1)
-    key = far * slots + lane
+    slot = lane % slots
+    code = source * 2 + far
     turn = jnp.zeros(grid.shape, jnp.int32)
-    for s in range(slots):
-        ahead = (source[:, s : s + 1] == source) & (key[:, s : s + 1] < key)
-        turn = turn + jnp.where(ahead, 1, 0)
+    for k in range(1, slots):
+        behind = pltpu.roll(code, k, 1)
+        ahead = pltpu.roll(code, LANES - k, 1)
+        same = (behind == code) | (behind == code - far)
+        turn = turn + jnp.where((slot >= k) & same, 1, 0)
+        turn = turn + jnp.where((slot + k < slots) & (far == 1) & (ahead == code - 1), 1, 0)
     most = slots // n_tensor
     local = matrix * per_rank + block
-    column = lax.broadcasted_iota(jnp.int32, picks_ref.shape, 1)
-    picks = jnp.zeros(picks_ref.shape, jnp.int32)
+    group_row = lax.broadcasted_iota(jnp.int32, (LANES, LANES), 0) // slots
+    group_column = lax.broadcasted_iota(jnp.int32, (LANES, LANES), 1)
+    picks = jnp.zeros(grid.shape, jnp.float32)
     for j in range(most):
-        chosen = jnp.where((source == me) & (turn == j), local, 0)
-        picks = jnp.where(column == j, jnp.sum(chosen, axis=1, keepdims=True), picks)
-    picks_ref[...] = picks
+        chosen = jnp.where((source == me) & (turn == j), local, 0).astype(jnp.float32)
+        spread = jnp.where(group_column == group_row * most + j, 1.0, 0.0)
+        picks = picks + jnp.dot(chosen, spread, preferred_element_type=jnp.float32)
+    picks_ref[...] = picks.astype(jnp.int32)
     where_ref[...] = source * most + turn
     wrong = jnp.where(turn < first_turns, far, 0)
     late_ref[...] = jnp.sum(jnp.sum(wrong, axis=1, keepdims=True), axis=0, keepdims=True)
 
 
 def exchange_kernel(n_data, n_tensor, per_rank, first_turns, picks_ref, offsets_ref, embed_ref, head_ref,
-                    incoming_ref, again_ref, rows, trail, near, far, ready, rest,
-                    load_sems, edge_send, edge_recv, send_sems, recv_sems):
+                    incoming_ref, again_ref, rows, trail, near, far, ready, rest, patched,
+                    load_sems, save_sem, edge_send, edge_recv, send_sems, recv_sems):
     data, rank = lax.axis_index("dp"), lax.axis_index("tensor")
     devices = n_data * n_tensor
     me = data * n_tensor + rank
@@ -83,6 +89,7 @@
     edge = trail.shape[1]
     most = incoming_ref.shape[0] // devices
     last_turns = most - first_turns
+    groups = LANES // (most * n_tensor)
     even = rank % 2 == 0
     near_rank = jnp.where(even, rank + 1, rank - 1)
     far_rank = jnp.where(even, (rank + n_tensor - 1) % n_tensor, (rank + 1) % n_tensor)
@@ -144,7 +151,7 @@
         return jnp.concatenate(tiles, axis=0), start - base * TILE
 
     def gathered(dest, j, with_far):
-        number = picks_ref[dest, j]
+        number = picks_ref[dest // groups, dest % groups * most + j]
         m = (number >= per_rank).astype(jnp.int32)
         first = (number - m * per_rank) * BLOCK
         low = jnp.where(m == 0, offsets_ref[0, rank], offsets_ref[1, rank]) - rank * span - first
@@ -172,13 +179,18 @@
             device_id=(d, t), device_id_type=MESH,
         )
 
+    def keep(phase, staged, count, base):
+        return pltpu.make_async_copy(
+            staged.at[pl.ds(me * count, count)], incoming_ref.at[pl.ds(me * most + base, count)], load_sems.at[phase]
+        )
+
     def wait_edge(which, target):
         copy = edge_copy(trail, target, which, near_rank)
         copy.wait_recv()
 
     def phase_of(phase, staged, count, base, with_far):
         for j in range(count):
-            incoming_ref[me * most + base + j] = gathered(me, base + j, with_far)
+            staged[me * count + j] = gathered(me, base + j, with_far)
 
         def one(k, carry):
             d, t = peer(k)
@@ -194,6 +206,7 @@
 
         lax.fori_loop(1, devices, one, 0)
         send(phase, staged, count, base, *peer(devices - 1)).start()
+        keep(phase, staged, count, base).start()
 
     wait_edge(0, near)
     if first_turns:
@@ -204,12 +217,13 @@
     if first_turns:
         def redo(to, carry):
             for j in range(first_turns):
-                again_ref[to * first_turns + j] = gathered(to, j, True)
+                patched[to * first_turns + j] = gathered(to, j, True)
             return carry
 
         lax.fori_loop(0, devices, redo, 0)
-    else:
-        again_ref[...] = jnp.zeros_like(again_ref)
+        save = pltpu.make_async_copy(patched, again_ref, save_sem)
+        save.start()
+        save.wait()
 
     edge_copy(trail, near, 0, near_rank).wait_send()
     edge_copy(trail, far, 1, far_rank).wait_send()
@@ -227,47 +241,110 @@
             return carry
 
         lax.fori_loop(1, devices, drain, 0)
+        keep(phase, staged, count, base).wait()
 
     if first_turns:
         finish_phase(0, ready, first_turns, 0)
     finish_phase(1, rest, last_turns, first_turns)
 
 
-def finish_kernel(n_data, n_tensor, per_step, where_ref, incoming_ref, probe_ref, stored_ref, sketch_ref):
+def finish_kernel(n_data, n_tensor, where_ref, incoming_ref, probe_ref, stored_ref, sketch_ref,
+                  slot_of, stored, sketch, load_sems, stored_sems, sketch_sems):
     width = incoming_ref.shape[2]
-    stride = incoming_ref.shape[0] // n_data
+    slots = stored_ref.shape[0]
+    most, groups = slots // n_tensor, LANES // slots
+    buffers = sketch.shape[0]
     me = lax.axis_index("dp") * n_tensor + lax.axis_index("tensor")
-    step = pl.program_id(0)
-    for q in range(per_step):
-        base = where_ref[me, step * per_step + q]
+    for t in range(n_tensor):
         for d in range(n_data):
-            stored_ref[q, :, d * width : (d + 1) * width] = incoming_ref[base + d * stride]
-    rows = stored_ref[...].reshape(per_step * BLOCK, n_data * width)
-    product = jnp.dot(rows, probe_ref[...], preferred_element_type=jnp.float32)
-    sketch_ref[...] = product.reshape(sketch_ref.shape)
-
-
-def plan(row_offsets, slot_grid, n_tensor, per_rank, first_turns):
-    devices, slots = slot_grid.shape
+            pltpu.make_async_copy(
+                incoming_ref.at[pl.ds((d * n_tensor + t) * most, most)],
+                stored.at[t, :, :, pl.ds(d * width, width)],
+                load_sems.at[t, d],
+            ).start()
+    for s in range(slots):
+        slot_of[where_ref[me // groups, me % groups * slots + s]] = s
+
+    def writes(t):
+        b = t % buffers
+        copies = []
+        for r in range(most):
+            slot = slot_of[t * most + r]
+            copies.append(pltpu.make_async_copy(sketch.at[b, r], sketch_ref.at[slot], sketch_sems.at[b, r]))
+            copies.append(pltpu.make_async_copy(stored.at[t, r], stored_ref.at[slot], stored_sems.at[t, r]))
+        return copies
+
+    for t in range(n_tensor):
+        b = t % buffers
+        for d in range(n_data):
+            pltpu.make_async_copy(
+                incoming_ref.at[pl.ds((d * n_tensor + t) * most, most)],
+                stored.at[t, :, :, pl.ds(d * width, width)],
+                load_sems.at[t, d],
+            ).wait()
+        if t >= buffers:
+            for write in writes(t - buffers):
+                write.wait()
+        rows = stored[t].reshape(most * BLOCK, n_data * width)
+        product = jnp.dot(rows, probe_ref[...], preferred_element_type=jnp.float32)
+        sketch[b] = product.reshape(sketch.shape[1:])
+        for write in writes(t):
+            write.start()
+    for t in range(max(n_tensor - buffers, 0), n_tensor):
+        for write in writes(t):
+            write.wait()
+
+
+def patch_kernel(n_data, n_tensor, first_turns, where_ref, fresh_ref, probe_ref, old_stored_ref, old_sketch_ref,
+                 stored_ref, sketch_ref, stored, sketch, sems):
+    width = fresh_ref.shape[2]
+    slots = stored_ref.shape[0]
+    most, groups = slots // n_tensor, LANES // slots
+    me = lax.axis_index("dp") * n_tensor + lax.axis_index("tensor")
+
+    def one(slot, carry):
+        base = where_ref[me // groups, me % groups * slots + slot]
+        turn = base % most
+
+        @pl.when(turn < first_turns)
+        def _():
+            for d in range(n_data):
+                held = (base // most + d * n_tensor) * first_turns + turn
+                stored[:, d * width : (d + 1) * width] = fresh_ref[held]
+            sketch[...] = jnp.dot(stored[...], probe_ref[...], preferred_element_type=jnp.float32)
+            writes = (
+                pltpu.make_async_copy(stored, stored_ref.at[slot], sems.at[0]),
+                pltpu.make_async_copy(sketch, sketch_ref.at[slot], sems.at[1]),
+            )
+            for write in writes:
+                write.start()
+            for write in writes:
+                write.wait()
+
+        return carry
+
+    lax.fori_loop(0, slots, one, 0)
+
+
+def plan(row_offsets, grid, n_tensor, per_rank, slots, first_turns):
     vmem = pl.BlockSpec(memory_space=pltpu.VMEM)
     return pl.pallas_call(
-        functools.partial(plan_kernel, n_tensor, per_rank, first_turns),
+        functools.partial(plan_kernel, n_tensor, per_rank, slots, first_turns),
         in_specs=[pl.BlockSpec(memory_space=pltpu.SMEM), vmem],
         out_specs=[vmem, vmem, vmem],
         out_shape=[
-            jax.ShapeDtypeStruct((devices, slots // n_tensor), jnp.int32),
-            jax.ShapeDtypeStruct((devices, slots), jnp.int32),
+            jax.ShapeDtypeStruct(grid.shape, jnp.int32),
+            jax.ShapeDtypeStruct(grid.shape, jnp.int32),
             jax.ShapeDtypeStruct((1, 1), jnp.int32),
         ],
         name="plan",
-    )(row_offsets, slot_grid)
-
-
-def exchange(picks, row_offsets, embed_rows, head_rows, n_data, n_tensor, per_rank, first_turns):
+    )(row_offsets, grid)
+
+
+def exchange(picks, row_offsets, embed_rows, head_rows, n_data, n_tensor, per_rank, most, first_turns):
     height, width = embed_rows.shape
     kind = embed_rows.dtype
     devices = n_data * n_tensor
-    most = picks.shape[1]
     edge = per_rank * BLOCK // 4 // TILE + 1
     smem = pl.BlockSpec(memory_space=pltpu.SMEM)
     vmem = pl.BlockSpec(memory_space=pltpu.VMEM)
@@ -275,7 +352,7 @@
     return pl.pallas_call(
         functools.partial(exchange_kernel, n_data, n_tensor, per_rank, first_turns),
         in_specs=[smem, smem, hbm, hbm],
-        out_specs=[vmem, vmem],
+        out_specs=[hbm, hbm],
         out_shape=[
             jax.ShapeDtypeStruct((devices * most, BLOCK, width), kind),
             jax.ShapeDtypeStruct((devices * max(first_turns, 1), BLOCK, width), kind),
@@ -287,14 +364,16 @@
             pltpu.VMEM((2, edge, TILE, width), kind),
             pltpu.VMEM((devices * max(first_turns, 1), BLOCK, width), kind),
             pltpu.VMEM((devices * (most - first_turns), BLOCK, width), kind),
+            pltpu.VMEM((devices * max(first_turns, 1), BLOCK, width), kind),
             pltpu.SemaphoreType.DMA((2,)),
+            pltpu.SemaphoreType.DMA,
             pltpu.SemaphoreType.DMA((2,)),
             pltpu.SemaphoreType.DMA((2,)),
             pltpu.SemaphoreType.DMA((2, devices)),
             pltpu.SemaphoreType.DMA((2, devices)),
         ],
         compiler_params=pltpu.CompilerParams(
-            collective_id=0, has_side_effects=True, vmem_limit_bytes=32 * MIB
+            collective_id=0, has_side_effects=True, vmem_limit_bytes=57 * MIB
         ),
         name="exchange",
     )(picks, row_offsets, embed_rows.reshape(-1, TILE, width), head_rows.reshape(-1, TILE, width))
@@ -302,31 +381,55 @@
 
 def finish(where, incoming, probe, n_data, n_tensor):
     columns, sketch_width = probe.shape
-    slot_count = where.shape[1]
-    per_step = 4
+    kind = incoming.dtype
+    slots = incoming.shape[0] // n_data
+    most = slots // n_tensor
+    buffers = 3
+    smem = pl.BlockSpec(memory_space=pltpu.SMEM)
+    vmem = pl.BlockSpec(memory_space=pltpu.VMEM)
+    hbm = pl.BlockSpec(memory_space=pltpu.HBM)
     return pl.pallas_call(
-        functools.partial(finish_kernel, n_data, n_tensor, per_step),
-        grid_spec=pltpu.PrefetchScalarGridSpec(
-            num_scalar_prefetch=1,
-            grid=(slot_count // per_step,),
-            in_specs=[
-                pl.BlockSpec(memory_space=pltpu.VMEM),
-                pl.BlockSpec(memory_space=pltpu.VMEM),
-            ],
-            out_specs=[
-                pl.BlockSpec((per_step, BLOCK, columns), lambda i, *_: (i, 0, 0)),
-                pl.BlockSpec((per_step, BLOCK, sketch_width), lambda i, *_: (i, 0, 0)),
-            ],
-        ),
+        functools.partial(finish_kernel, n_data, n_tensor),
+        in_specs=[smem, hbm, vmem],
+        out_specs=[hbm, hbm],
         out_shape=[
-            jax.ShapeDtypeStruct((slot_count, BLOCK, columns), incoming.dtype),
-            jax.ShapeDtypeStruct((slot_count, BLOCK, sketch_width), jnp.float32),
-        ],
-        compiler_params=pltpu.CompilerParams(
-            dimension_semantics=("arbitrary",), vmem_limit_bytes=32 * MIB
-        ),
+            jax.ShapeDtypeStruct((slots, BLOCK, columns), kind),
+            jax.ShapeDtypeStruct((slots, BLOCK, sketch_width), jnp.float32),
+        ],
+        scratch_shapes=[
+            pltpu.SMEM((slots,), jnp.int32),
+            pltpu.VMEM((n_tensor, most, BLOCK, columns), kind),
+            pltpu.VMEM((buffers, most, BLOCK, sketch_width), jnp.float32),
+            pltpu.SemaphoreType.DMA((n_tensor, n_data)),
+            pltpu.SemaphoreType.DMA((n_tensor, most)),
+            pltpu.SemaphoreType.DMA((buffers, most)),
+        ],
+        compiler_params=pltpu.CompilerParams(vmem_limit_bytes=57 * MIB),
         name="finish",
     )(where, incoming, probe)
+
+
+def patch(where, fresh, probe, stored, sketch, n_data, n_tensor, first_turns):
+    smem = pl.BlockSpec(memory_space=pltpu.SMEM)
+    vmem = pl.BlockSpec(memory_space=pltpu.VMEM)
+    hbm = pl.BlockSpec(memory_space=pltpu.HBM)
+    return pl.pallas_call(
+        functools.partial(patch_kernel, n_data, n_tensor, first_turns),
+        in_specs=[smem, vmem, vmem, hbm, hbm],
+        out_specs=[hbm, hbm],
+        out_shape=[
+            jax.ShapeDtypeStruct(stored.shape, stored.dtype),
+            jax.ShapeDtypeStruct(sketch.shape, sketch.dtype),
+        ],
+        scratch_shapes=[
+            pltpu.VMEM(stored.shape[1:], stored.dtype),
+            pltpu.VMEM(sketch.shape[1:], sketch.dtype),
+            pltpu.SemaphoreType.DMA((2,)),
+        ],
+        input_output_aliases={3: 0, 4: 1},
+        compiler_params=pltpu.CompilerParams(vmem_limit_bytes=32 * MIB),
+        name="patch",
+    )(where, fresh, probe, stored, sketch)
 
 
 def shards(embed_rows, head_rows, row_offsets, slot_table, probe):
@@ -336,23 +439,23 @@
     slots = slot_table.shape[0] // devices
     most = slots // n_tensor
     first_turns = most // 4
-    picks, where, late = plan(row_offsets, slot_table.reshape(devices, slots), n_tensor, per_rank, first_turns)
-    incoming, again = exchange(picks, row_offsets, embed_rows, head_rows, n_data, n_tensor, per_rank, first_turns)
-
-    def ended(where, incoming, again, probe):
-        return tuple(finish(where, incoming, probe, n_data, n_tensor))
-
-    def resent(where, incoming, again, probe):
+    picks, where, late = plan(row_offsets, slot_table.reshape(-1, LANES), n_tensor, per_rank, slots, first_turns)
+    incoming, again = exchange(
+        picks, row_offsets, embed_rows, head_rows, n_data, n_tensor, per_rank, most, first_turns
+    )
+
+    stored, sketch = finish(where, incoming, probe, n_data, n_tensor)
+    if not first_turns:
+        return stored, sketch
+
+    def kept(where, again, probe, stored, sketch):
+        return stored, sketch
+
+    def resent(where, again, probe, stored, sketch):
         fresh = lax.all_to_all(again, AXES, split_axis=0, concat_axis=0, tiled=True)
-        shape = incoming.shape
-        fresh = fresh.reshape((devices, first_turns) + shape[1:])
-        held = incoming.reshape((devices, most) + shape[1:])
-        whole = jnp.concatenate([fresh, held[:, first_turns:]], axis=1).reshape(shape)
-        return ended(where, whole, again, probe)
-
-    if not first_turns:
-        return ended(where, incoming, again, probe)
-    return lax.cond(late[0, 0] == 0, ended, resent, where, incoming, again, probe)
+        return tuple(patch(where, fresh, probe, stored, sketch, n_data, n_tensor, first_turns))
+
+    return lax.cond(late[0, 0] == 0, kept, resent, where, again, probe, stored, sketch)
 
 
 def solution(mesh):

time: 136 us -> 127 us (0.934)
  local copies, waits for them, and re-layouts: 6.53 us -> 0.01 us
  Pallas kernels: 128 us -> 125 us
    unnamed x8 -> x2, local copies, waits for them, and re-layouts: 5.17 us -> 0.01 us
    pallas_call x2, Pallas kernels: 14.2 us -> 11.7 us  [the longest x1 9.95 us: finish(): pl.pallas_call(functools.partial(finish_kernel, n_data, n_tensor), in_spe...]
    reshape x1 -> x0, local copies, waits for them, and re-layouts: 1.36 us -> none  [shards(): slot_table.reshape(devices, slots)]
where the time goes in v2:
time: 127 us; the launch traced here: 126 us
  Pallas kernels  125 us (98%)
  between operations  1.32 us (1%)
    pallas_call x1, Pallas kernels, exchange(): pl.pallas_call(functools.partial(exchange_kernel, n_data, n_tensor, per_r...  113 us
    pallas_call x1, Pallas kernels, finish(): pl.pallas_call(functools.partial(finish_kernel, n_data, n_tensor), in_spe...  9.95 us

profile of v2, /device:TPU:0, one launch (start us, length us, event | category | flops | bytes accessed | tf_op | source)
XLA Modules:
  0.0 126.4 jit_solution(9765117809665599971)
XLA Ops:
  0.6 0.0 copy-start
  0.6 1.7 %plan.1 = (s32[8,128]{1,0:T(8,128)}, s32[8,128]{1,0:T(8,128)S(1)}, s32[1,1]{1,0:T(1,128)}) custom-call(s32[2,9]{1,0:T(2,128)} %offsets_ref.3, s32[8,128]{1,0:T(8,128)} %bitcast.6), custom_call_target="tpu_custom_call" | custom-call | tf_op jit(solution)/shard_map/plan/pallas_call | solution.py:331
  3.0 113.4 %exchange.1 = (bf16[128,128,128]{2,1,0:T(8,128)(2,1)}, bf16[32,128,128]{2,1,0:T(8,128)(2,1)S(1)}) custom-call(s32[8,128]{1,0:T(8,128)} %get-tuple-element.29.picks_ref, s32[2,9]{1,0:T(2,128)} %offsets_ref.3, bf16[768,16,128]{2,1,0:T(8,128)(2,1)} %bitcast.4, bf16[768,16,128]{2,1,0:T(8,128)(2,1)} %bitcast.5), custom_call_target="tpu_custom_call" | custom-call | tf_op jit(solution)/shard_map/exchange/pallas_call | solution.py:352
  116.4 0.0 copy-done
  116.5 10.0 %finish.1 = (bf16[32,128,512]{2,1,0:T(8,128)(2,1)}, f32[32,128,1024]{2,1,0:T(8,128)}) custom-call(s32[8,128]{1,0:T(8,128)S(1)} %get-tuple-element.31.where_ref, bf16[128,128,128]{2,1,0:T(8,128)(2,1)} %get-tuple-element.32.incoming_ref, bf16[512,1024]{1,0:T(8,128)(2,1)S(1)} %copy-done), custom_call_target="tpu_custom_call" | custom-call | tf_op jit(solution)/shard_map/finish/pallas_call | solution.py:391
  (1 shorter events, 0.0 us)
Async XLA Ops:
  0.6 115.8 %copy-start = (bf16[512,1024]{1,0:T(8,128)(2,1)S(1)}, bf16[512,1024]{1,0:T(8,128)(2,1)}, u32[]{:S(2)}) copy-start(bf16[512,1024]{1,0:T(8,128)(2,1)} %probe_ref.1) | copy-start | bytes 3145732

commit v3 on v2

--- a/solution.py
+++ b/solution.py
@@ -20,6 +20,10 @@
     return lax.shift_right_arithmetic(value, 4)
 
 
+def shallow_tiles(span):
+    return 5 * (span // 4) // 8 // TILE
+
+
 def tail_begin(offset, rank, span, height):
     return jnp.clip((rank + 1) * span - offset, 0, height - span // 4 - 1)
 
@@ -34,7 +38,7 @@
     return jnp.dot(selector(offset), window, preferred_element_type=jnp.float32)
 
 
-def plan_kernel(n_tensor, per_rank, slots, first_turns, offsets_ref, grid_ref, picks_ref, where_ref, late_ref):
+def plan_kernel(n_tensor, per_rank, slots, turns, offsets_ref, grid_ref, picks_ref, where_ref, *late_refs):
     me = lax.axis_index("tensor")
     span = per_rank * BLOCK
     grid = grid_ref[...]
@@ -44,25 +48,30 @@
     source = lax.shift_right_logical(within, per_rank.bit_length() - 1)
     block = within - source * per_rank
     first = block * BLOCK
-    far = jnp.zeros(grid.shape, jnp.int32)
+    shallow = shallow_tiles(span) * TILE
+    level = jnp.zeros(grid.shape, jnp.int32)
     for m in range(2):
         for t in range(n_tensor):
             if t % 2 == 0:
-                touched = first < offsets_ref[m, t] - t * span
+                low = offsets_ref[m, t] - t * span
+                touched = first < low
+                need = jnp.minimum(first + BLOCK, low) + TILE
             else:
-                touched = first + BLOCK > offsets_ref[m, t + 1] - t * span
-            here = (source == t) & (matrix == m)
-            far = far + jnp.where(here & touched, 1, 0)
+                high = offsets_ref[m, t + 1] - t * span
+                touched = first + BLOCK > high
+                need = first + BLOCK - high
+            here = (source == t) & (matrix == m) & touched
+            level = level + jnp.where(here, jnp.where(need > shallow, 2, 1), 0)
     lane = lax.broadcasted_iota(jnp.int32, grid.shape, 1)
     slot = lane % slots
-    code = source * 2 + far
+    code = source * 4 + level
+    floor = source * 4
     turn = jnp.zeros(grid.shape, jnp.int32)
     for k in range(1, slots):
         behind = pltpu.roll(code, k, 1)
         ahead = pltpu.roll(code, LANES - k, 1)
-        same = (behind == code) | (behind == code - far)
-        turn = turn + jnp.where((slot >= k) & same, 1, 0)
-        turn = turn + jnp.where((slot + k < slots) & (far == 1) & (ahead == code - 1), 1, 0)
+        turn = turn + jnp.where((slot >= k) & (behind >= floor) & (behind <= code), 1, 0)
+        turn = turn + jnp.where((slot + k < slots) & (ahead >= floor) & (ahead < code), 1, 0)
     most = slots // n_tensor
     local = matrix * per_rank + block
     group_row = lax.broadcasted_iota(jnp.int32, (LANES, LANES), 0) // slots
@@ -74,13 +83,15 @@
         picks = picks + jnp.dot(chosen, spread, preferred_element_type=jnp.float32)
     picks_ref[...] = picks.astype(jnp.int32)
     where_ref[...] = source * most + turn
-    wrong = jnp.where(turn < first_turns, far, 0)
-    late_ref[...] = jnp.sum(jnp.sum(wrong, axis=1, keepdims=True), axis=0, keepdims=True)
-
-
-def exchange_kernel(n_data, n_tensor, per_rank, first_turns, picks_ref, offsets_ref, embed_ref, head_ref,
-                    incoming_ref, again_ref, rows, trail, near, far, ready, rest, patched,
-                    load_sems, save_sem, edge_send, edge_recv, send_sems, recv_sems):
+    for phase, late_ref in enumerate(late_refs):
+        ours = (turn >= sum(turns[:phase])) & (turn < sum(turns[: phase + 1]))
+        wrong = jnp.where(ours & (level > phase), 1, 0)
+        late_ref[...] = jnp.sum(jnp.sum(wrong, axis=1, keepdims=True), axis=0, keepdims=True)
+
+
+def exchange_kernel(n_data, n_tensor, per_rank, turns, picks_ref, offsets_ref, embed_ref, head_ref,
+                    incoming_ref, again_ref, again_second_ref, rows, trail, near, shallow, far, ready, second, rest, patched, patched_second,
+                    load_sems, save_sem, keep_sems, edge_send, edge_recv, send_sems, recv_sems):
     data, rank = lax.axis_index("dp"), lax.axis_index("tensor")
     devices = n_data * n_tensor
     me = data * n_tensor + rank
@@ -88,7 +99,7 @@
     height = rows.shape[1] * TILE
     edge = trail.shape[1]
     most = incoming_ref.shape[0] // devices
-    last_turns = most - first_turns
+    cut = shallow.shape[1]
     groups = LANES // (most * n_tensor)
     even = rank % 2 == 0
     near_rank = jnp.where(even, rank + 1, rank - 1)
@@ -125,23 +136,25 @@
     lax.fori_loop(0, edge, fill, 0)
     pl.semaphore_wait(barrier, devices - 1)
 
-    lead = rows.at[:, pl.ds(0, edge)]
-
     def edge_copy(source, target, which, t):
         return pltpu.make_async_remote_copy(
             src_ref=source, dst_ref=target, send_sem=edge_send.at[which], recv_sem=edge_recv.at[which],
             device_id=(data, t), device_id_type=MESH,
         )
 
+    whole, upper, lower = pl.ds(0, edge), pl.ds(0, cut), pl.ds(cut, edge - cut)
+
     @pl.when(even)
     def _():
         edge_copy(trail, near, 0, near_rank).start()
-        edge_copy(lead, far, 1, far_rank).start()
+        edge_copy(rows.at[:, upper], shallow, 1, far_rank).start()
+        edge_copy(rows.at[:, lower], far.at[:, lower], 2, far_rank).start()
 
     @pl.when(jnp.logical_not(even))
     def _():
-        edge_copy(lead, near, 0, near_rank).start()
-        edge_copy(trail, far, 1, far_rank).start()
+        edge_copy(rows.at[:, whole], near, 0, near_rank).start()
+        edge_copy(trail.at[:, upper], shallow, 1, far_rank).start()
+        edge_copy(trail.at[:, lower], far.at[:, lower], 2, far_rank).start()
 
     row = lax.broadcasted_iota(jnp.int32, (BLOCK, rows.shape[3]), 0)
 
@@ -150,7 +163,7 @@
         tiles = [buffer[m, base + i] for i in range(WINDOW // TILE)]
         return jnp.concatenate(tiles, axis=0), start - base * TILE
 
-    def gathered(dest, j, with_far):
+    def gathered(dest, j, beyond):
         number = picks_ref[dest // groups, dest % groups * most + j]
         m = (number >= per_rank).astype(jnp.int32)
         first = (number - m * per_rank) * BLOCK
@@ -161,9 +174,9 @@
         from_left = first + left_begin - tile_of(left_begin) * TILE
         from_right = -high
         piece, offset = window(near, m, jnp.where(even, from_right, from_left))
-        if with_far:
+        if beyond is not None:
             use_far = jnp.where(even, low > 0, high < BLOCK)
-            other, other_offset = window(far, m, jnp.where(even, from_left, from_right))
+            other, other_offset = window(beyond, m, jnp.where(even, from_left, from_right))
             piece = jnp.where(use_far, other, piece)
             offset = jnp.where(use_far, other_offset, offset)
         kept = moved(own_offset, own)
@@ -181,22 +194,24 @@
 
     def keep(phase, staged, count, base):
         return pltpu.make_async_copy(
-            staged.at[pl.ds(me * count, count)], incoming_ref.at[pl.ds(me * most + base, count)], load_sems.at[phase]
+            staged.at[pl.ds(me * count, count)], incoming_ref.at[pl.ds(me * most + base, count)], keep_sems.at[phase]
         )
 
-    def wait_edge(which, target):
-        copy = edge_copy(trail, target, which, near_rank)
-        copy.wait_recv()
-
-    def phase_of(phase, staged, count, base, with_far):
+    edge_copies = [
+        edge_copy(trail, near, 0, near_rank),
+        edge_copy(trail.at[:, upper], shallow, 1, far_rank),
+        edge_copy(trail.at[:, lower], far.at[:, lower], 2, far_rank),
+    ]
+
+    def phase_of(phase, staged, count, base, beyond):
         for j in range(count):
-            staged[me * count + j] = gathered(me, base + j, with_far)
+            staged[me * count + j] = gathered(me, base + j, beyond)
 
         def one(k, carry):
             d, t = peer(k)
             to = d * n_tensor + t
             for j in range(count):
-                staged[to * count + j] = gathered(to, base + j, with_far)
+                staged[to * count + j] = gathered(to, base + j, beyond)
 
             @pl.when(k > 1)
             def _():
@@ -208,25 +223,40 @@
         send(phase, staged, count, base, *peer(devices - 1)).start()
         keep(phase, staged, count, base).start()
 
-    wait_edge(0, near)
-    if first_turns:
-        phase_of(0, ready, first_turns, 0, False)
-    wait_edge(1, far)
-    phase_of(1, rest, last_turns, first_turns, True)
-
-    if first_turns:
-        def redo(to, carry):
-            for j in range(first_turns):
-                patched[to * first_turns + j] = gathered(to, j, True)
-            return carry
-
-        lax.fori_loop(0, devices, redo, 0)
-        save = pltpu.make_async_copy(patched, again_ref, save_sem)
-        save.start()
-        save.wait()
-
-    edge_copy(trail, near, 0, near_rank).wait_send()
-    edge_copy(trail, far, 1, far_rank).wait_send()
+    phases = [
+        (phase, staged, count, sum(turns[:phase]), beyond)
+        for phase, (staged, count, beyond) in enumerate(zip((ready, second, rest), turns, (None, shallow, far)))
+        if count
+    ]
+
+    def join(i, carry):
+        for m in range(2):
+            far[m, i] = shallow[m, i]
+        return carry
+
+    for phase in range(3):
+        edge_copies[phase].wait_recv()
+        if phase == 2:
+            lax.fori_loop(0, cut, join, 0)
+        for entry in phases:
+            if entry[0] == phase:
+                phase_of(*entry)
+
+    for entry, fixed, again in zip(phases, (patched, patched_second), (again_ref, again_second_ref)):
+        phase, _, count, base, _ = entry
+        if phase < 2:
+            def redo(to, carry, fixed=fixed, count=count, base=base):
+                for j in range(count):
+                    fixed[to * count + j] = gathered(to, base + j, far)
+                return carry
+
+            lax.fori_loop(0, devices, redo, 0)
+            save = pltpu.make_async_copy(fixed, again, save_sem)
+            save.start()
+            save.wait()
+
+    for copy in edge_copies:
+        copy.wait_send()
 
     def finish_phase(phase, staged, count, base):
         def drain(k, carry):
@@ -243,9 +273,8 @@
         lax.fori_loop(1, devices, drain, 0)
         keep(phase, staged, count, base).wait()
 
-    if first_turns:
-        finish_phase(0, ready, first_turns, 0)
-    finish_phase(1, rest, last_turns, first_turns)
+    for entry in phases:
+        finish_phase(*entry[:4])
 
 
 def finish_kernel(n_data, n_tensor, where_ref, incoming_ref, probe_ref, stored_ref, sketch_ref,
@@ -295,7 +324,7 @@
             write.wait()
 
 
-def patch_kernel(n_data, n_tensor, first_turns, where_ref, fresh_ref, probe_ref, old_stored_ref, old_sketch_ref,
+def patch_kernel(n_data, n_tensor, begin, count, where_ref, fresh_ref, probe_ref, old_stored_ref, old_sketch_ref,
                  stored_ref, sketch_ref, stored, sketch, sems):
     width = fresh_ref.shape[2]
     slots = stored_ref.shape[0]
@@ -306,10 +335,10 @@
         base = where_ref[me // groups, me % groups * slots + slot]
         turn = base % most
 
-        @pl.when(turn < first_turns)
+        @pl.when((turn >= begin) & (turn < begin + count))
         def _():
             for d in range(n_data):
-                held = (base // most + d * n_tensor) * first_turns + turn
+                held = (base // most + d * n_tensor) * count + turn - begin
                 stored[:, d * width : (d + 1) * width] = fresh_ref[held]
             sketch[...] = jnp.dot(stored[...], probe_ref[...], preferred_element_type=jnp.float32)
             writes = (
@@ -326,51 +355,63 @@
     lax.fori_loop(0, slots, one, 0)
 
 
-def plan(row_offsets, grid, n_tensor, per_rank, slots, first_turns):
+def plan(row_offsets, grid, n_tensor, per_rank, slots, turns):
     vmem = pl.BlockSpec(memory_space=pltpu.VMEM)
     return pl.pallas_call(
-        functools.partial(plan_kernel, n_tensor, per_rank, slots, first_turns),
+        functools.partial(plan_kernel, n_tensor, per_rank, slots, turns),
         in_specs=[pl.BlockSpec(memory_space=pltpu.SMEM), vmem],
-        out_specs=[vmem, vmem, vmem],
+        out_specs=[vmem, vmem, vmem, vmem],
         out_shape=[
             jax.ShapeDtypeStruct(grid.shape, jnp.int32),
             jax.ShapeDtypeStruct(grid.shape, jnp.int32),
             jax.ShapeDtypeStruct((1, 1), jnp.int32),
+            jax.ShapeDtypeStruct((1, 1), jnp.int32),
         ],
         name="plan",
     )(row_offsets, grid)
 
 
-def exchange(picks, row_offsets, embed_rows, head_rows, n_data, n_tensor, per_rank, most, first_turns):
+def exchange(picks, row_offsets, embed_rows, head_rows, n_data, n_tensor, per_rank, most, turns):
     height, width = embed_rows.shape
     kind = embed_rows.dtype
     devices = n_data * n_tensor
     edge = per_rank * BLOCK // 4 // TILE + 1
     smem = pl.BlockSpec(memory_space=pltpu.SMEM)
-    vmem = pl.BlockSpec(memory_space=pltpu.VMEM)
     hbm = pl.BlockSpec(memory_space=pltpu.HBM)
+
+    def blocks(count):
+        return pltpu.VMEM((devices * max(count, 1), BLOCK, width), kind)
+
+    def tiles(count):
+        return pltpu.VMEM((2, count, TILE, width), kind)
+
     return pl.pallas_call(
-        functools.partial(exchange_kernel, n_data, n_tensor, per_rank, first_turns),
+        functools.partial(exchange_kernel, n_data, n_tensor, per_rank, turns),
         in_specs=[smem, smem, hbm, hbm],
-        out_specs=[hbm, hbm],
+        out_specs=[hbm, hbm, hbm],
         out_shape=[
             jax.ShapeDtypeStruct((devices * most, BLOCK, width), kind),
-            jax.ShapeDtypeStruct((devices * max(first_turns, 1), BLOCK, width), kind),
+            jax.ShapeDtypeStruct((devices * max(turns[0], 1), BLOCK, width), kind),
+            jax.ShapeDtypeStruct((devices * max(turns[1], 1), BLOCK, width), kind),
         ],
         scratch_shapes=[
-            pltpu.VMEM((2, height // TILE, TILE, width), kind),
-            pltpu.VMEM((2, edge, TILE, width), kind),
-            pltpu.VMEM((2, edge, TILE, width), kind),
-            pltpu.VMEM((2, edge, TILE, width), kind),
-            pltpu.VMEM((devices * max(first_turns, 1), BLOCK, width), kind),
-            pltpu.VMEM((devices * (most - first_turns), BLOCK, width), kind),
-            pltpu.VMEM((devices * max(first_turns, 1), BLOCK, width), kind),
+            tiles(height // TILE),
+            tiles(edge),
+            tiles(edge),
+            tiles(shallow_tiles(per_rank * BLOCK)),
+            tiles(edge),
+            blocks(turns[0]),
+            blocks(turns[1]),
+            blocks(turns[2]),
+            blocks(turns[0]),
+            blocks(turns[1]),
             pltpu.SemaphoreType.DMA((2,)),
             pltpu.SemaphoreType.DMA,
-            pltpu.SemaphoreType.DMA((2,)),
-            pltpu.SemaphoreType.DMA((2,)),
-            pltpu.SemaphoreType.DMA((2, devices)),
-            pltpu.SemaphoreType.DMA((2, devices)),
+            pltpu.SemaphoreType.DMA((3,)),
+            pltpu.SemaphoreType.DMA((3,)),
+            pltpu.SemaphoreType.DMA((3,)),
+            pltpu.SemaphoreType.DMA((3, devices)),
+            pltpu.SemaphoreType.DMA((3, devices)),
         ],
         compiler_params=pltpu.CompilerParams(
             collective_id=0, has_side_effects=True, vmem_limit_bytes=57 * MIB
@@ -409,12 +450,12 @@
     )(where, incoming, probe)
 
 
-def patch(where, fresh, probe, stored, sketch, n_data, n_tensor, first_turns):
+def patch(where, fresh, probe, stored, sketch, n_data, n_tensor, begin, count):
     smem = pl.BlockSpec(memory_space=pltpu.SMEM)
     vmem = pl.BlockSpec(memory_space=pltpu.VMEM)
     hbm = pl.BlockSpec(memory_space=pltpu.HBM)
     return pl.pallas_call(
-        functools.partial(patch_kernel, n_data, n_tensor, first_turns),
+        functools.partial(patch_kernel, n_data, n_tensor, begin, count),
         in_specs=[smem, vmem, vmem, hbm, hbm],
         out_specs=[hbm, hbm],
         out_shape=[
@@ -438,24 +479,25 @@
     per_rank = slot_table.shape[0] // (2 * n_tensor)
     slots = slot_table.shape[0] // devices
     most = slots // n_tensor
-    first_turns = most // 4
-    picks, where, late = plan(row_offsets, slot_table.reshape(-1, LANES), n_tensor, per_rank, slots, first_turns)
-    incoming, again = exchange(
-        picks, row_offsets, embed_rows, head_rows, n_data, n_tensor, per_rank, most, first_turns
+    turns = (most // 4, most // 4, most - 2 * (most // 4))
+    picks, where, *late = plan(row_offsets, slot_table.reshape(-1, LANES), n_tensor, per_rank, slots, turns)
+    incoming, *again = exchange(
+        picks, row_offsets, embed_rows, head_rows, n_data, n_tensor, per_rank, most, turns
     )
-
-    stored, sketch = finish(where, incoming, probe, n_data, n_tensor)
-    if not first_turns:
-        return stored, sketch
-
-    def kept(where, again, probe, stored, sketch):
-        return stored, sketch
-
-    def resent(where, again, probe, stored, sketch):
+    result = tuple(finish(where, incoming, probe, n_data, n_tensor))
+
+    def kept(where, again, probe, result):
+        return result
+
+    def resent(begin, count, where, again, probe, result):
         fresh = lax.all_to_all(again, AXES, split_axis=0, concat_axis=0, tiled=True)
-        return tuple(patch(where, fresh, probe, stored, sketch, n_data, n_tensor, first_turns))
-
-    return lax.cond(late[0, 0] == 0, kept, resent, where, again, probe, stored, sketch)
+        return tuple(patch(where, fresh, probe, *result, n_data, n_tensor, begin, count))
+
+    for phase in range(2):
+        if turns[phase]:
+            other = functools.partial(resent, sum(turns[:phase]), turns[phase])
+            result = lax.cond(late[phase][0, 0] == 0, kept, other, where, again[phase], probe, result)
+    return result
 
 
 def solution(mesh):

time: 127 us -> 119 us (0.937)
  Pallas kernels: 125 us -> 116 us
    pallas_call x1, Pallas kernels: 113 us -> 105 us  [exchange(): pl.pallas_call(functools.partial(exchange_kernel, n_data, n_tensor, per_r...]
where the time goes in v3:
time: 119 us; the launch traced here: 118 us
  Pallas kernels  116 us (97%)
  between operations  2.01 us (2%)
    pallas_call x1, Pallas kernels, exchange(): pl.pallas_call(functools.partial(exchange_kernel, n_data, n_tensor, per_r...  105 us
    pallas_call x1, Pallas kernels, finish(): pl.pallas_call(functools.partial(finish_kernel, n_data, n_tensor), in_spe...  9.95 us

profile of v3, /device:TPU:0, one launch (start us, length us, event | category | flops | bytes accessed | tf_op | source)
XLA Modules:
  0.0 118.5 jit_solution(12930513512495572197)
XLA Ops:
  0.6 0.0 copy-start
  0.6 1.7 %plan.1 = (s32[8,128]{1,0:T(8,128)}, s32[8,128]{1,0:T(8,128)S(1)}, s32[1,1]{1,0:T(1,128)}, s32[1,1]{1,0:T(1,128)}) custom-call(s32[2,9]{1,0:T(2,128)} %offsets_ref.3, s32[8,128]{1,0:T(8,128)} %bitcast.7), custom_call_target="tpu_custom_call" | custom-call | tf_op jit(solution)/shard_map/plan/pallas_call | solution.py:360
  3.7 104.8 %exchange.1 = (bf16[128,128,128]{2,1,0:T(8,128)(2,1)}, bf16[32,128,128]{2,1,0:T(8,128)(2,1)S(1)}, bf16[32,128,128]{2,1,0:T(8,128)(2,1)S(1)}) custom-call(s32[8,128]{1,0:T(8,128)} %get-tuple-element.52.picks_ref, s32[2,9]{1,0:T(2,128)} %offsets_ref.3, bf16[768,16,128]{2,1,0:T(8,128)(2,1)} %bitcast.5, bf16[768,16,128]{2,1,0:T(8,128)(2,1)} %bitcast.6), custom_call_target="tpu_custom_call" | custom-call | tf_op jit(solution)/shard_map/exchange/pallas_call | solution.py:388
  108.5 0.0 copy-done
  108.5 10.0 %finish.1 = (bf16[32,128,512]{2,1,0:T(8,128)(2,1)}, f32[32,128,1024]{2,1,0:T(8,128)}) custom-call(s32[8,128]{1,0:T(8,128)S(1)} %get-tuple-element.54.where_ref, bf16[128,128,128]{2,1,0:T(8,128)(2,1)} %get-tuple-element.57.incoming_ref, bf16[512,1024]{1,0:T(8,128)(2,1)S(1)} %copy-done), custom_call_target="tpu_custom_call" | custom-call | tf_op jit(solution)/shard_map/finish/pallas_call | solution.py:432
  (2 shorter events, 0.0 us)
Async XLA Ops:
  0.6 107.8 %copy-start = (bf16[512,1024]{1,0:T(8,128)(2,1)S(1)}, bf16[512,1024]{1,0:T(8,128)(2,1)}, u32[]{:S(2)}) copy-start(bf16[512,1024]{1,0:T(8,128)(2,1)} %probe_ref.1) | copy-start | bytes 3145732

commit v4 on v3

--- a/solution.py
+++ b/solution.py
@@ -38,10 +38,8 @@
     return jnp.dot(selector(offset), window, preferred_element_type=jnp.float32)
 
 
-def plan_kernel(n_tensor, per_rank, slots, turns, offsets_ref, grid_ref, picks_ref, where_ref, *late_refs):
-    me = lax.axis_index("tensor")
+def plan(me, n_tensor, per_rank, slots, turns, offsets_ref, grid):
     span = per_rank * BLOCK
-    grid = grid_ref[...]
     total = n_tensor * per_rank
     matrix = (grid >= total).astype(jnp.int32)
     within = grid - matrix * total
@@ -81,17 +79,19 @@
         chosen = jnp.where((source == me) & (turn == j), local, 0).astype(jnp.float32)
         spread = jnp.where(group_column == group_row * most + j, 1.0, 0.0)
         picks = picks + jnp.dot(chosen, spread, preferred_element_type=jnp.float32)
-    picks_ref[...] = picks.astype(jnp.int32)
-    where_ref[...] = source * most + turn
-    for phase, late_ref in enumerate(late_refs):
+    late = jnp.zeros(grid.shape, jnp.int32)
+    for phase in range(2):
         ours = (turn >= sum(turns[:phase])) & (turn < sum(turns[: phase + 1]))
         wrong = jnp.where(ours & (level > phase), 1, 0)
-        late_ref[...] = jnp.sum(jnp.sum(wrong, axis=1, keepdims=True), axis=0, keepdims=True)
-
-
-def exchange_kernel(n_data, n_tensor, per_rank, turns, picks_ref, offsets_ref, embed_ref, head_ref,
-                    incoming_ref, again_ref, again_second_ref, rows, trail, near, shallow, far, ready, second, rest, patched, patched_second,
-                    load_sems, save_sem, keep_sems, edge_send, edge_recv, send_sems, recv_sems):
+        wrong = jnp.sum(jnp.sum(wrong, axis=1, keepdims=True), axis=0, keepdims=True)
+        late = jnp.where(lane == phase, wrong, late)
+    return picks.astype(jnp.int32), source * most + turn, late
+
+
+def exchange_kernel(n_data, n_tensor, per_rank, turns, offsets_ref, table_ref, embed_ref, head_ref,
+                    incoming_ref, again_ref, again_second_ref, where_ref, late_ref,
+                    table, notes, picks, rows, trail, near, shallow, far, ready, second, rest, patched, patched_second,
+                    load_sems, note_sems, save_sem, keep_sems, edge_send, edge_recv, send_sems, recv_sems):
     data, rank = lax.axis_index("dp"), lax.axis_index("tensor")
     devices = n_data * n_tensor
     me = data * n_tensor + rank
@@ -110,6 +110,8 @@
         pltpu.make_async_copy(buffer, rows.at[m], load_sems.at[m])
         for m, buffer in enumerate((embed_ref, head_ref))
     ]
+    read = pltpu.make_async_copy(table_ref, table, note_sems.at[0])
+    read.start()
     for load in loads:
         load.start()
 
@@ -125,6 +127,10 @@
 
     lax.fori_loop(1, devices, greet, 0)
 
+    read.wait()
+    found = plan(rank, n_tensor, per_rank, most * n_tensor, turns, offsets_ref, table[...])
+    for i in range(3):
+        notes[i] = found[i]
     for load in loads:
         load.wait()
 
@@ -134,6 +140,10 @@
         return carry
 
     lax.fori_loop(0, edge, fill, 0)
+    note = pltpu.make_async_copy(notes, picks, note_sems.at[0])
+    note.start()
+    pass_on = pltpu.make_async_copy(notes.at[1], where_ref, note_sems.at[1])
+    pass_on.start()
     pl.semaphore_wait(barrier, devices - 1)
 
     def edge_copy(source, target, which, t):
@@ -164,7 +174,7 @@
         return jnp.concatenate(tiles, axis=0), start - base * TILE
 
     def gathered(dest, j, beyond):
-        number = picks_ref[dest // groups, dest % groups * most + j]
+        number = picks[0, dest // groups, dest % groups * most + j]
         m = (number >= per_rank).astype(jnp.int32)
         first = (number - m * per_rank) * BLOCK
         low = jnp.where(m == 0, offsets_ref[0, rank], offsets_ref[1, rank]) - rank * span - first
@@ -234,6 +244,9 @@
             far[m, i] = shallow[m, i]
         return carry
 
+    note.wait()
+    pass_on.wait()
+    late_ref[0, 0] = jnp.minimum(picks[2, 0, 0], 1) + 2 * jnp.minimum(picks[2, 0, 1], 1)
     for phase in range(3):
         edge_copies[phase].wait_recv()
         if phase == 2:
@@ -355,23 +368,7 @@
     lax.fori_loop(0, slots, one, 0)
 
 
-def plan(row_offsets, grid, n_tensor, per_rank, slots, turns):
-    vmem = pl.BlockSpec(memory_space=pltpu.VMEM)
-    return pl.pallas_call(
-        functools.partial(plan_kernel, n_tensor, per_rank, slots, turns),
-        in_specs=[pl.BlockSpec(memory_space=pltpu.SMEM), vmem],
-        out_specs=[vmem, vmem, vmem, vmem],
-        out_shape=[
-            jax.ShapeDtypeStruct(grid.shape, jnp.int32),
-            jax.ShapeDtypeStruct(grid.shape, jnp.int32),
-            jax.ShapeDtypeStruct((1, 1), jnp.int32),
-            jax.ShapeDtypeStruct((1, 1), jnp.int32),
-        ],
-        name="plan",
-    )(row_offsets, grid)
-
-
-def exchange(picks, row_offsets, embed_rows, head_rows, n_data, n_tensor, per_rank, most, turns):
+def exchange(row_offsets, table, embed_rows, head_rows, n_data, n_tensor, per_rank, most, turns):
     height, width = embed_rows.shape
     kind = embed_rows.dtype
     devices = n_data * n_tensor
@@ -387,14 +384,19 @@
 
     return pl.pallas_call(
         functools.partial(exchange_kernel, n_data, n_tensor, per_rank, turns),
-        in_specs=[smem, smem, hbm, hbm],
-        out_specs=[hbm, hbm, hbm],
+        in_specs=[smem, hbm, hbm, hbm],
+        out_specs=[hbm, hbm, hbm, hbm, smem],
         out_shape=[
             jax.ShapeDtypeStruct((devices * most, BLOCK, width), kind),
             jax.ShapeDtypeStruct((devices * max(turns[0], 1), BLOCK, width), kind),
             jax.ShapeDtypeStruct((devices * max(turns[1], 1), BLOCK, width), kind),
+            jax.ShapeDtypeStruct(table.shape, jnp.int32),
+            jax.ShapeDtypeStruct((1, 1), jnp.int32),
         ],
         scratch_shapes=[
+            pltpu.VMEM(table.shape, jnp.int32),
+            pltpu.VMEM((3,) + table.shape, jnp.int32),
+            pltpu.SMEM((3,) + table.shape, jnp.int32),
             tiles(height // TILE),
             tiles(edge),
             tiles(edge),
@@ -405,6 +407,7 @@
             blocks(turns[2]),
             blocks(turns[0]),
             blocks(turns[1]),
+            pltpu.SemaphoreType.DMA((2,)),
             pltpu.SemaphoreType.DMA((2,)),
             pltpu.SemaphoreType.DMA,
             pltpu.SemaphoreType.DMA((3,)),
@@ -417,7 +420,7 @@
             collective_id=0, has_side_effects=True, vmem_limit_bytes=57 * MIB
         ),
         name="exchange",
-    )(picks, row_offsets, embed_rows.reshape(-1, TILE, width), head_rows.reshape(-1, TILE, width))
+    )(row_offsets, table, embed_rows.reshape(-1, TILE, width), head_rows.reshape(-1, TILE, width))
 
 
 def finish(where, incoming, probe, n_data, n_tensor):
@@ -480,24 +483,28 @@
     slots = slot_table.shape[0] // devices
     most = slots // n_tensor
     turns = (most // 4, most // 4, most - 2 * (most // 4))
-    picks, where, *late = plan(row_offsets, slot_table.reshape(-1, LANES), n_tensor, per_rank, slots, turns)
-    incoming, *again = exchange(
-        picks, row_offsets, embed_rows, head_rows, n_data, n_tensor, per_rank, most, turns
+    incoming, first, second, where, late = exchange(
+        row_offsets, slot_table.reshape(-1, LANES), embed_rows, head_rows, n_data, n_tensor, per_rank, most, turns
     )
+    again = (first, second)
     result = tuple(finish(where, incoming, probe, n_data, n_tensor))
 
     def kept(where, again, probe, result):
         return result
 
-    def resent(begin, count, where, again, probe, result):
-        fresh = lax.all_to_all(again, AXES, split_axis=0, concat_axis=0, tiled=True)
+    def resent(begin, count, phase, where, again, probe, result):
+        fresh = lax.all_to_all(again[phase], AXES, split_axis=0, concat_axis=0, tiled=True)
         return tuple(patch(where, fresh, probe, *result, n_data, n_tensor, begin, count))
 
-    for phase in range(2):
-        if turns[phase]:
-            other = functools.partial(resent, sum(turns[:phase]), turns[phase])
-            result = lax.cond(late[phase][0, 0] == 0, kept, other, where, again[phase], probe, result)
-    return result
+    def both(*args):
+        return redone[1](*args[:-1], redone[0](*args))
+
+    redone = [
+        functools.partial(resent, sum(turns[:phase]), turns[phase], phase) for phase in range(2)
+    ]
+    if not turns[0]:
+        return result
+    return lax.switch(late[0, 0], [kept, *redone, both], where, again, probe, result)
 
 
 def solution(mesh):

time: 119 us -> 117 us (0.983)
    pallas_call x1 -> x0, Pallas kernels: 1.73 us -> none  [plan(): pl.pallas_call(functools.partial(plan_kernel, n_tensor, per_rank, slots,...]
where the time goes in v4:
time: 117 us
  Pallas kernels  115 us (98%)
  between operations  1.24 us (1%)
    pallas_call x1, Pallas kernels, exchange(): pl.pallas_call(functools.partial(exchange_kernel, n_data, n_tensor, per_r...  105 us
    pallas_call x1, Pallas kernels, finish(): pl.pallas_call(functools.partial(finish_kernel, n_data, n_tensor), in_spe...  9.95 us

profile of v4, /device:TPU:0, one launch (start us, length us, event | category | flops | bytes accessed | tf_op | source)
XLA Modules:
  0.0 116.6 jit_solution(11506855288629000780)
XLA Ops:
  0.6 0.0 copy-start
  0.6 105.4 %exchange.1 = (bf16[128,128,128]{2,1,0:T(8,128)(2,1)}, bf16[32,128,128]{2,1,0:T(8,128)(2,1)S(1)}, bf16[32,128,128]{2,1,0:T(8,128)(2,1)}, s32[8,128]{1,0:T(8,128)S(1)}, s32[1,1]{1,0:T(1,128)}) custom-call(s32[2,9]{1,0:T(2,128)} %offsets_ref.1, s32[8,128]{1,0:T(8,128)} %bitcast.6, bf16[768,16,128]{2,1,0:T(8,128)(2,1)} %bitcast.4, bf16[768,16,128]{2,1,0:T(8,128)(2,1)} %bitcast.5), custom_call_target="tpu_custom_call" | custom-call | tf_op jit(solution)/shard_map/exchange/pallas_call | solution.py:385
  106.0 0.0 copy-done
  106.0 10.0 %finish.1 = (bf16[32,128,512]{2,1,0:T(8,128)(2,1)}, f32[32,128,1024]{2,1,0:T(8,128)}) custom-call(s32[8,128]{1,0:T(8,128)S(1)} %get-tuple-element.64.where_ref, bf16[128,128,128]{2,1,0:T(8,128)(2,1)} %get-tuple-element.65.incoming_ref, bf16[512,1024]{1,0:T(8,128)(2,1)S(1)} %copy-done), custom_call_target="tpu_custom_call" | custom-call | tf_op jit(solution)/shard_map/finish/pallas_call | solution.py:435
  (1 shorter events, 0.0 us)
Async XLA Ops:
  0.6 105.4 %copy-start = (bf16[512,1024]{1,0:T(8,128)(2,1)S(1)}, bf16[512,1024]{1,0:T(8,128)(2,1)}, u32[]{:S(2)}) copy-start(bf16[512,1024]{1,0:T(8,128)(2,1)} %probe_ref.1) | copy-start | bytes 3145732

commit v5 on v4

--- a/solution.py
+++ b/solution.py
@@ -88,9 +88,9 @@
     return picks.astype(jnp.int32), source * most + turn, late
 
 
-def exchange_kernel(n_data, n_tensor, per_rank, turns, offsets_ref, table_ref, embed_ref, head_ref,
+def exchange_kernel(n_data, n_tensor, per_rank, turns, starts_ref, table_ref, embed_ref, head_ref,
                     incoming_ref, again_ref, again_second_ref, where_ref, late_ref,
-                    table, notes, picks, rows, trail, near, shallow, far, ready, second, rest, patched, patched_second,
+                    offsets_ref, table, notes, picks, rows, trail, near, shallow, far, ready, second, rest, patched, patched_second,
                     load_sems, note_sems, save_sem, keep_sems, edge_send, edge_recv, send_sems, recv_sems):
     data, rank = lax.axis_index("dp"), lax.axis_index("tensor")
     devices = n_data * n_tensor
@@ -112,6 +112,8 @@
     ]
     read = pltpu.make_async_copy(table_ref, table, note_sems.at[0])
     read.start()
+    starts = pltpu.make_async_copy(starts_ref, offsets_ref, note_sems.at[1])
+    starts.start()
     for load in loads:
         load.start()
 
@@ -128,6 +130,7 @@
     lax.fori_loop(1, devices, greet, 0)
 
     read.wait()
+    starts.wait()
     found = plan(rank, n_tensor, per_rank, most * n_tensor, turns, offsets_ref, table[...])
     for i in range(3):
         notes[i] = found[i]
@@ -290,13 +293,15 @@
         finish_phase(*entry[:4])
 
 
-def finish_kernel(n_data, n_tensor, where_ref, incoming_ref, probe_ref, stored_ref, sketch_ref,
-                  slot_of, stored, sketch, load_sems, stored_sems, sketch_sems):
+def finish_kernel(n_data, n_tensor, places_ref, incoming_ref, probe_ref, stored_ref, sketch_ref,
+                  where_ref, slot_of, stored, sketch, place_sem, load_sems, stored_sems, sketch_sems):
     width = incoming_ref.shape[2]
     slots = stored_ref.shape[0]
     most, groups = slots // n_tensor, LANES // slots
     buffers = sketch.shape[0]
     me = lax.axis_index("dp") * n_tensor + lax.axis_index("tensor")
+    places = pltpu.make_async_copy(places_ref, where_ref, place_sem)
+    places.start()
     for t in range(n_tensor):
         for d in range(n_data):
             pltpu.make_async_copy(
@@ -304,6 +309,7 @@
                 stored.at[t, :, :, pl.ds(d * width, width)],
                 load_sems.at[t, d],
             ).start()
+    places.wait()
     for s in range(slots):
         slot_of[where_ref[me // groups, me % groups * slots + s]] = s
 
@@ -384,7 +390,7 @@
 
     return pl.pallas_call(
         functools.partial(exchange_kernel, n_data, n_tensor, per_rank, turns),
-        in_specs=[smem, hbm, hbm, hbm],
+        in_specs=[hbm, hbm, hbm, hbm],
         out_specs=[hbm, hbm, hbm, hbm, smem],
         out_shape=[
             jax.ShapeDtypeStruct((devices * most, BLOCK, width), kind),
@@ -394,6 +400,7 @@
             jax.ShapeDtypeStruct((1, 1), jnp.int32),
         ],
         scratch_shapes=[
+            pltpu.SMEM(row_offsets.shape, jnp.int32),
             pltpu.VMEM(table.shape, jnp.int32),
             pltpu.VMEM((3,) + table.shape, jnp.int32),
             pltpu.SMEM((3,) + table.shape, jnp.int32),
@@ -429,21 +436,22 @@
     slots = incoming.shape[0] // n_data
     most = slots // n_tensor
     buffers = 3
-    smem = pl.BlockSpec(memory_space=pltpu.SMEM)
     vmem = pl.BlockSpec(memory_space=pltpu.VMEM)
     hbm = pl.BlockSpec(memory_space=pltpu.HBM)
     return pl.pallas_call(
         functools.partial(finish_kernel, n_data, n_tensor),
-        in_specs=[smem, hbm, vmem],
+        in_specs=[hbm, hbm, vmem],
         out_specs=[hbm, hbm],
         out_shape=[
             jax.ShapeDtypeStruct((slots, BLOCK, columns), kind),
             jax.ShapeDtypeStruct((slots, BLOCK, sketch_width), jnp.float32),
         ],
         scratch_shapes=[
+            pltpu.SMEM(where.shape, jnp.int32),
             pltpu.SMEM((slots,), jnp.int32),
             pltpu.VMEM((n_tensor, most, BLOCK, columns), kind),
             pltpu.VMEM((buffers, most, BLOCK, sketch_width), jnp.float32),
+            pltpu.SemaphoreType.DMA,
             pltpu.SemaphoreType.DMA((n_tensor, n_data)),
             pltpu.SemaphoreType.DMA((n_tensor, most)),
             pltpu.SemaphoreType.DMA((buffers, most)),

time: 117 us -> 116 us (level)
  no operation moved by 1% of the time
where the time goes in v5:
time: 116 us; the launch traced here: 115 us
  Pallas kernels  114 us (98%)
  between operations  1.24 us (1%)
    pallas_call x1, Pallas kernels, exchange(): pl.pallas_call(functools.partial(exchange_kernel, n_data, n_tensor, per_r...  105 us
    pallas_call x1, Pallas kernels, finish(): pl.pallas_call(functools.partial(finish_kernel, n_data, n_tensor), in_spe...  9.36 us

profile of v5, /device:TPU:0, one launch (start us, length us, event | category | flops | bytes accessed | tf_op | source)
XLA Modules:
  0.0 115.2 jit_solution(14711013503163684942)
XLA Ops:
  0.6 0.0 copy-start
  0.6 104.6 %exchange.1 = (bf16[128,128,128]{2,1,0:T(8,128)(2,1)}, bf16[32,128,128]{2,1,0:T(8,128)(2,1)S(1)}, bf16[32,128,128]{2,1,0:T(8,128)(2,1)}, s32[8,128]{1,0:T(8,128)S(1)}, s32[1,1]{1,0:T(1,128)}) custom-call(s32[2,9]{1,0:T(2,128)} %starts_ref.1, s32[8,128]{1,0:T(8,128)} %bitcast.6, bf16[768,16,128]{2,1,0:T(8,128)(2,1)} %bitcast.4, bf16[768,16,128]{2,1,0:T(8,128)(2,1)} %bitcast.5), custom_call_target="tpu_custom_call" | custom-call | tf_op jit(solution)/shard_map/exchange/pallas_call | solution.py:391
  105.3 0.0 copy-done
  105.3 9.4 %finish.1 = (bf16[32,128,512]{2,1,0:T(8,128)(2,1)}, f32[32,128,1024]{2,1,0:T(8,128)}) custom-call(s32[8,128]{1,0:T(8,128)S(1)} %get-tuple-element.64.places_ref, bf16[128,128,128]{2,1,0:T(8,128)(2,1)} %get-tuple-element.65.incoming_ref, bf16[512,1024]{1,0:T(8,128)(2,1)S(1)} %copy-done), custom_call_target="tpu_custom_call" | custom-call | tf_op jit(solution)/shard_map/finish/pallas_call | solution.py:441
  (1 shorter events, 0.0 us)
Async XLA Ops:
  0.6 104.6 %copy-start = (bf16[512,1024]{1,0:T(8,128)(2,1)S(1)}, bf16[512,1024]{1,0:T(8,128)(2,1)}, u32[]{:S(2)}) copy-start(bf16[512,1024]{1,0:T(8,128)(2,1)} %probe_ref.1) | copy-start | bytes 3145732
